TPU v7x, 32 devices: a whole 2x2x4 slice. The times are simulated.
32 devices in a mesh: band: 8 (over z, y), grid: 4 (over x, core).
Axes of the slice: x: 2, y: 2, z: 4, core: 2. Of those that a mesh axis runs over, the one named last changes fastest.
Arguments:
- orbitals: float32 [32, 110592], P('band', 'grid'), may hold values from -6 to 6
Outputs:
- exchange_vectors: float32 [32, 110592], P('band', 'grid')
- margin: float32 [32, 32], P('grid', 'band')
All inputs are finite; a program needn't handle non-finite values.
Results may differ from a plain program's by a relative error of at most 0.00012.
Values sent between devices are 32-bit elements; how exact they have to be, the bound alone decides.
A program may use at most 128 MiB of HBM per device.

v0:
```python
import functools

import jax
import jax.numpy as jnp
import numpy as np
from jax import lax
from jax.experimental import pallas as pl
from jax.experimental.pallas import tpu as pltpu
from jax.sharding import PartitionSpec as P


def kernel_values(ng):
    freqs = ((np.arange(ng) + ng // 2) % ng - ng // 2).astype(np.float32)
    sq = freqs[: ng // 2 + 1, None, None] ** 2 + freqs[None, :, None] ** 2 + freqs[None, None, :] ** 2
    safe = np.where(sq > 0, sq, np.float32(1.0))
    return np.where(sq > 0, 40.0 * (1.0 - np.exp(-sq / 16.0)) / safe, 0.0)


def hartley(ng):
    k = np.arange(ng)
    ang = (k[:, None] * k[None, :] % ng) * (2.0 * np.pi / ng)
    return np.cos(ang) + np.sin(ang)


def split_const(table):
    table = np.asarray(table, np.float32)
    hi = table.astype(jnp.bfloat16)
    lo = (table - hi.astype(np.float32)).astype(jnp.bfloat16)
    return hi, lo


def rfft(xs):
    n = len(xs)
    if n == 3:
        s = xs[1] + xs[2]
        d = xs[1] - xs[2]
        return [(xs[0] + s, None), (xs[0] - 0.5 * s, d * (-np.sqrt(3.0) / 2))]
    even, odd = rfft(xs[0::2]), rfft(xs[1::2])
    half = n // 2
    out = [None] * (half + 1)
    for k in range(half // 2 + 1):
        er, ei = even[k]
        orr, oi = odd[k]
        if k == 0:
            out[0] = (er + orr, None)
            out[half] = (er - orr, None)
            continue
        c, s = np.cos(2 * np.pi * k / n), -np.sin(2 * np.pi * k / n)
        if 2 * k == half:
            out[k] = (er, -orr)
            continue
        tr, ti = cmul(orr, oi, c, s)
        out[k] = (er + tr, addo(ei, ti))
        out[half - k] = (er - tr, subo(ti, ei))
    return out


def addo(a, b):
    return b if a is None else a + b


def subo(a, b):
    return a if b is None else a - b


def cmul(r, i, c, s):
    if i is None:
        return r * c, r * s
    if abs(abs(c) - abs(s)) < 1e-9:
        if s < 0 < c:
            return (r + i) * c, (i - r) * c
        return (r - i) * c, (r + i) * c
    return r * c - i * s, r * s + i * c


def irfft(spec, n):
    if n == 3:
        dc, (r, i) = spec[0][0], spec[1]
        base = dc - r
        t = i * np.sqrt(3.0)
        return [dc + 2.0 * r, base - t, base + t]
    half = n // 2
    even, odd = [None] * (half // 2 + 1), [None] * (half // 2 + 1)
    for k in range(half // 2 + 1):
        yr, yi = spec[k]
        if k == 0:
            hr = spec[half][0]
            even[0] = (yr + hr, None)
            odd[0] = (yr - hr, None)
            continue
        if 2 * k == half:
            even[k] = (yr + yr, None)
            odd[k] = (-(yi + yi), None)
            continue
        zr, zi = spec[half - k]
        er, ei = yr + zr, yi - zi
        dr, di = yr - zr, yi + zi
        c, s = np.cos(2 * np.pi * k / n), np.sin(2 * np.pi * k / n)
        even[k] = (er, ei)
        odd[k] = cmul(dr, di, c, s)
    ev, od = irfft(even, half), irfft(odd, half)
    out = [None] * n
    out[0::2], out[1::2] = ev, od
    return out


def split(v):
    hi = v.astype(jnp.bfloat16)
    lo = (v - hi.astype(jnp.float32)).astype(jnp.bfloat16)
    return hi, lo


def mm(a, b):
    return jnp.dot(a, b, preferred_element_type=jnp.float32)


def solve_kernel(ng, own_ref, k1_ref, k2_ref, zh_ref, zl_ref, ty_ref, sel_ref, s_ref, o_ref,
                 buf, amp, acc, work, vec, recv, rsem, ssem, nsem, osem, orsem, lsem):
    planes, _, width = own_ref.shape
    me = lax.axis_index("grid")
    band, nband = lax.axis_index("band"), lax.axis_size("band")
    chip, core = me // 2, me % 2
    sib = chip * 2 + (1 - core)
    cross = (1 - chip) * 2 + core
    far = (1 - chip) * 2 + (1 - core)
    above, below = (band + 1) % nband, (band + nband - 1) % nband
    mesh_id = pl.DeviceIdType.MESH

    def remote(src, dst, send, recv_sem, device):
        return pltpu.make_async_remote_copy(
            src_ref=src, dst_ref=dst, send_sem=send, recv_sem=recv_sem,
            device_id=device, device_id_type=mesh_id,
        )

    def share(blk, lane, slot, src, target):
        return remote(src, buf.at[blk, slot], ssem.at[blk, lane], rsem.at[blk, slot], (band, target))

    barrier = pltpu.get_barrier_semaphore()
    for device in ((band, sib), (band, cross), (band, far), (above, me), (below, me)):
        pl.semaphore_signal(barrier, inc=1, device_id=device, device_id_type=mesh_id)
    pl.semaphore_wait(barrier, 5)

    share(0, 1, me, own_ref, cross).start()
    share(0, 0, me, own_ref, sib).start()
    remote(own_ref, buf.at[1, me], nsem.at[0], rsem.at[1, me], (above, me)).start()
    remote(own_ref, buf.at[2, me], nsem.at[1], rsem.at[2, me], (below, me)).start()
    local = pltpu.make_async_copy(own_ref, buf.at[0, me], lsem)
    local.start()

    def arrived(blk, slot):
        share(blk, 0, slot, own_ref, sib).wait_recv()

    def relay(blk):
        arrived(blk, cross)
        share(blk, 2, cross, buf.at[blk, cross], sib).start()

    def spread(blk):
        arrived(blk, me)
        share(blk, 1, me, buf.at[blk, me], cross).start()
        share(blk, 0, me, buf.at[blk, me], sib).start()

    def ztrans(v):
        hi, lo = split(v)
        return mm(hi, zh_ref[...]) + mm(lo, zh_ref[...]) + mm(hi, zl_ref[...])

    def ytrans(v):
        hi, lo = split(v)
        return mm(ty_ref[...], jnp.concatenate([hi, lo, hi], axis=0))

    def slot_of(s):
        return ((chip + s // 2) % 2) * 2 + (core + s % 2) % 2

    def amplitude(slot):
        hi, lo = split(buf[0, slot].reshape(planes * ng, width))
        amp[slot] = (mm(hi, sel_ref[me]) + mm(lo, sel_ref[me])).reshape(planes, ng, width)

    def forward(blk, s):
        slot = slot_of(s)

        @pl.when(s == 1)
        def _():
            arrived(blk, sib)

        @pl.when(jnp.logical_and(blk == 0, s == 2))
        def _():
            relay(0)
            spread(1)

        @pl.when(s == 3)
        def _():
            arrived(blk, far)

        @pl.when(blk == 0)
        def _():
            amplitude(slot)

        p = (amp[slot] * buf[blk, slot]).reshape(planes * ng, width)
        q = ztrans(p).reshape(planes, ng, width)
        for r in range(planes):
            work[slot, r] = ytrans(q[r])

    def conv(vals, kern):
        spec = rfft(vals)
        out = []
        for k, (re, im) in enumerate(spec):
            kv = kern(k)
            out.append((re * kv, None if im is None else im * kv))
        return irfft(out, ng)

    def xconv(t):
        order = [(g, h, r) for g in range(4) for h in range(2) for r in range(planes)]
        for i in range(2):
            rows = pl.ds(pl.multiple_of(t * 16 + 8 * i, 8), 8)
            res = conv([work[g, r, rows, h * 128:h * 128 + 128] for g, h, r in order],
                       lambda k: k1_ref[k, rows, :])
            for (g, h, r), v in zip(order, res):
                work[g, r, rows, h * 128:h * 128 + 128] = v
        ra = pl.ds(pl.multiple_of(t * 16, 8), 8)
        rb = pl.ds(pl.multiple_of(t * 16 + 8, 8), 8)
        left = lax.broadcasted_iota(jnp.int32, (8, 128), 1) < 64

        def half(g, h, r):
            u, w = work[g, r, ra, 256:384], work[g, r, rb, 256:384]
            if h == 0:
                return jnp.where(left, u, pltpu.roll(w, 64, 1))
            return jnp.where(left, pltpu.roll(u, 64, 1), w)

        rk = pl.ds(pl.multiple_of(t * 8, 8), 8)
        res = dict(zip(order, conv([half(*o) for o in order], lambda k: k2_ref[k, rk, :])))
        for g in range(4):
            for r in range(planes):
                a, b = res[(g, 0, r)], res[(g, 1, r)]
                work[g, r, ra, 256:384] = jnp.where(left, a, pltpu.roll(b, 64, 1))
                work[g, r, rb, 256:384] = jnp.where(left, pltpu.roll(a, 64, 1), b)

    def push(slot):
        return remote(vec.at[slot], recv.at[me], osem.at[slot], orsem.at[me], (band, slot))

    def inverse(blk, s):
        slot = ((chip + 1 - s // 2) % 2) * 2 + (core + s % 2 + s // 2) % 2
        q = jnp.concatenate([ytrans(work[slot, r]) for r in range(planes)], axis=0)
        w = ztrans(q).reshape(planes, ng, width) * buf[blk, slot]

        @pl.when(blk == 0)
        def _():
            acc[slot] = w

        @pl.when(blk == 1)
        def _():
            acc[slot] += w

        @pl.when(blk == 2)
        def _():
            hi, lo = split((acc[slot] + w).reshape(planes * ng, width))
            out = -(mm(hi, s_ref[...]) + mm(lo, s_ref[...]))
            vec[slot] = out.reshape(planes, ng, s_ref.shape[-1])

            @pl.when(s < 3)
            def _():
                push(slot).start()

    def block(blk, _):
        @pl.when(blk == 0)
        def _():
            local.wait()

        @pl.when(blk > 0)
        def _():
            relay(blk)

        @pl.when(blk == 1)
        def _():
            spread(2)

        def fwd(s, _):
            forward(blk, s)
            return 0

        def mid(t, _):
            xconv(t)
            return 0

        def inv(s, _):
            inverse(blk, s)
            return 0

        lax.fori_loop(0, 4, fwd, 0)
        lax.fori_loop(0, ng // 16, mid, 0)
        lax.fori_loop(0, 4, inv, 0)
        return 0

    lax.fori_loop(0, 3, block, 0)

    o_ref[me] = vec[me]
    for slot in (sib, cross, far):
        remote(vec.at[slot], recv.at[slot], osem.at[slot], orsem.at[slot], (band, slot)).wait()
        o_ref[slot] = recv[slot]
    for blk in range(3):
        for lane, target in ((0, sib), (1, cross), (2, sib)):
            share(blk, lane, me, own_ref, target).wait_send()
    remote(own_ref, buf.at[1, me], nsem.at[0], rsem.at[1, me], (above, me)).wait_send()
    remote(own_ref, buf.at[2, me], nsem.at[1], rsem.at[2, me], (below, me)).wait_send()


def lane_tables(ng, bands):
    w = bands * ng
    half, bz = [], []
    for lo, hi in ((0, 128), (128, w)):
        for h in range(2):
            half.append(np.full(hi - lo, h))
            bz.append(np.arange(lo, hi))
    half, bz = np.concatenate(half), np.concatenate(bz)
    return half, bz // ng, bz % ng


def solve(own, bands, groups):
    planes, ng, width = own.shape
    half, bnd, zed = lane_tables(ng, bands)
    ht = hartley(ng)
    th, tl = split_const(ht)
    same = (half[:, None] == half[None, :])
    zh, zl = split_const(np.where(same & (bnd[:, None] == bnd[None, :]), ht[zed[:, None], zed[None, :]], 0.0))
    ty = np.concatenate([th, th, tl], axis=1)
    copyz = same & (zed[:, None] == zed[None, :])
    sel = np.stack([copyz & (bnd[:, None] == g) for g in range(groups)]).astype(np.float32)
    s = np.zeros((width, 128), np.float32)
    s[np.arange(width), half * ng + zed] = 1.0
    kv = kernel_values(ng).astype(np.float32) / np.float32(ng**3)
    kb = np.tile(kv, (1, 1, bands))
    k1 = kb[:, :, :128]
    rest = kb[:, :, 128:].reshape(kb.shape[0], ng // 16, 2, 8, 64)
    k2 = np.concatenate([rest[:, :, 0], rest[:, :, 1]], axis=-1).reshape(kb.shape[0], ng // 2, 128)
    consts = [k1, k2, zh, zl, ty, sel.astype(jnp.bfloat16), s.astype(jnp.bfloat16)]
    full = (groups, planes, ng, width)
    f32, dma = jnp.float32, pltpu.SemaphoreType.DMA
    return pl.pallas_call(
        functools.partial(solve_kernel, ng),
        out_shape=jax.ShapeDtypeStruct((groups, planes, ng, 128), f32),
        in_specs=[pl.BlockSpec(memory_space=pltpu.VMEM)] * 8,
        out_specs=pl.BlockSpec(memory_space=pltpu.VMEM),
        scratch_shapes=[
            pltpu.VMEM((3,) + full, f32), pltpu.VMEM(full, f32), pltpu.VMEM(full, f32), pltpu.VMEM(full, f32),
            pltpu.VMEM((groups, planes, ng, 128), f32), pltpu.VMEM((groups, planes, ng, 128), f32),
            dma((3, groups)), dma((3, 3)), dma((2,)), dma((groups,)), dma((groups,)), dma(()),
        ],
        compiler_params=pltpu.CompilerParams(
            vmem_limit_bytes=56 * 1024 * 1024, collective_id=0, has_side_effects=True
        ),
        cost_estimate=pl.CostEstimate(flops=10**11, bytes_accessed=10**7, transcendentals=0),
        name="solve",
    )(own, *[jnp.asarray(c) for c in consts])


def on_device(orbitals):
    groups = lax.axis_size("grid")
    bands, local = orbitals.shape
    ncell = local * groups
    ng = round(ncell ** (1 / 3))
    xs = local // (ng * ng)
    planes = xs // 2
    t = orbitals.reshape(bands, 2, planes, ng, ng).transpose(2, 3, 1, 0, 4).reshape(planes, ng, 2, bands * ng)
    own = jnp.concatenate([t[:, :, 0, :128], t[:, :, 1, :128], t[:, :, 0, 128:], t[:, :, 1, 128:]], axis=-1)
    out = solve(own, bands, groups)
    vec = out[..., : 2 * ng].reshape(groups, planes, ng, 2, ng).transpose(0, 3, 1, 2, 4)
    vectors = vec.reshape(bands, local)
    terms = (
        lax.dot_general(
            lax.all_gather(orbitals, "band", axis=0, tiled=True),
            vectors,
            (((1,), (1,)), ((), ())),
            precision=lax.Precision.HIGHEST,
            preferred_element_type=jnp.float32,
        )
        / ncell
    )
    margin = lax.psum_scatter(terms, "grid", scatter_dimension=0, tiled=True)
    return (vectors, margin)


def solution(mesh):
    return jax.shard_map(
        on_device,
        mesh=mesh,
        in_specs=(P("band", "grid"),),
        out_specs=(P("band", "grid"), P("grid", "band")),
        check_vma=False,
    )
```

profile of v0, /device:TPU:0, one launch (start us, length us, event | category | flops | bytes accessed | tf_op | source)
XLA Modules:
  0.0 107.4 jit_solution(13691321328897510730)
XLA Ops:
  7.2 0.0 all-gather.3.cloned.1.call-start
  7.2 0.7 all-gather.3.cloned.1.call-update
  7.9 1.6 %reshape.16 = f32[4,2,6,48,48]{4,3,2,1,0:T(8,128)S(1)} reshape(f32[4,27648]{1,0:T(4,128)} %param.8) | data formatting | bytes 884736 | tf_op jit(solution)/shard_map/reshape | solution.py:361
  9.5 0.8 copy.17
  10.2 0.5 reshape.17
  10.8 0.9 pad_maximum_fusion.own_ref
  11.7 58.7 %solve.1 = f32[4,6,48,128]{3,2,1,0:T(8,128)} custom-call(f32[6,48,384]{2,1,0:T(8,128)} %pad_maximum_fusion.own_ref, f32[25,48,128]{2,1,0:T(8,128)} %constant.17.clone.k1_ref, f32[25,24,128]{2,1,0:T(8,128)} %constant.18.clone.k2_ref, bf16[384,384]{1,0:T(8,128)(2,1)} %constant.19.clone.zh_ref, bf16[384,384]{1,0:T(8,128)(2,1)} %constant.20.clone.zl_ref, ...), custom_call_target="tpu_custom_call" | custom-call | flops 99999997952 | bytes 10000000 | tf_op jit(solution)/shard_map/solve/pallas_call | solution.py:336
  70.4 0.0 copy-start
  70.4 1.7 %reshape.18 = f32[4,6,48,2,48]{4,3,2,1,0:T(2,128)S(1)} reshape(f32[4,6,48,96]{3,2,1,0:T(8,128)} %bitcast.30) | data formatting | bytes 884736 | tf_op jit(solution)/shard_map/reshape | solution.py:364
  72.1 0.1 copy.13
  72.2 1.6 %reshape.19 = f32[4,27648]{1,0:T(4,128)} reshape(f32[4,2,6,48,48]{4,3,2,1,0:T(8,128)S(1)} %copy.13) | data formatting | bytes 884736 | tf_op jit(solution)/shard_map/reshape | solution.py:365
  73.8 0.0 copy-done
  73.8 0.6 dynamic-slice
  75.0 12.6 %all-gather.3.cloned.1.call-done = f32[8,4,27648]{2,1,0:T(4,128)} async-done(((f32[1,4,27648]{2,1,0:T(4,128)}), f32[8,4,27648]{2,1,0:T(4,128)}) %all-gather.3.cloned.1.call-update) | async-done | bytes 3538960 | tf_op jit(solution)/shard_map/all_gather | solution.py:368
  87.7 2.7 %reshape.21 = f32[32,27648]{1,0:T(8,128)S(1)} reshape(f32[8,4,27648]{2,1,0:T(4,128)} %all-gather.3.cloned.1.call-done) | data formatting | bytes 7077888
  90.4 3.8 %fusion = f32[32,4]{0,1:T(4,128)S(1)} fusion(f32[4,27648]{1,0:T(4,128)} %reshape.19, f32[32,27648]{1,0:T(8,128)S(1)} %reshape.21), kind=kOutput, calls=%fused_computation.2 | convolution fusion | flops 42467456 | bytes 3981824 | tf_op jit(solution)/shard_map/dot_general | solution.py:367
  94.3 5.7 %all-reduce = f32[32,4]{0,1:T(4,128)S(1)} all-reduce(f32[32,4]{0,1:T(4,128)S(1)} %fusion), channel_id=2, replica_groups=mesh['band'=8,'grid'=4] {'grid'}, use_global_device_ids=true, to_apply=%region_0.0.clone | all-reduce | flops 128 | bytes 1024
  99.9 0.7 constant_dynamic-slice_fusion
  (2 shorter events, 0.0 us)
Async XLA Ops:
  7.2 80.5 %all-gather.3.cloned.1.call-start = ((), (), s32[]{:S(2)}) async-start(), calls=%async_computation | async-start | bytes 3981312 | tf_op jit(solution)/shard_map/all_gather | solution.py:368
  70.4 3.4 %copy-start = (u32[32]{0:T(128)S(1)}, u32[32]{0:T(128)}, u32[]{:S(2)}) copy-start(u32[32]{0:T(128)} %constant.27) | copy-start | bytes 388
Sparse Core Ops, SparseCore 0:
  10.2 77.4 all-gather.2
where the time goes:
time: 108 us; the launch traced here: 107 us
  Pallas kernels  58.7 us (54%)
  between operations  14.8 us (14%)
  waiting for transfers between devices  13.3 us (12%)
  local copies, waits for them, and re-layouts  10.3 us (10%)
  blocking collectives  5.65 us (5%)
  matrix products  3.85 us (4%)
    pallas_call x1, Pallas kernels, solve(): pl.pallas_call(functools.partial(solve_kernel, ng), out_shape=jax.ShapeDt...  58.7 us
    all_gather x1, waiting for transfers between devices, on_device(): lax.all_gather(orbitals, 'band', axis=0, tiled=True)  12.6 us
    unnamed x1, blocking collectives  5.65 us
    unnamed x5, local copies, waits for them, and re-layouts  3.96 us
    dot_general x1, matrix products, on_device(): lax.dot_general(lax.all_gather(orbitals, 'band', axis=0, tiled=True), vec...  3.85 us
    reshape x3, local copies, waits for them, and re-layouts, on_device(): orbitals.reshape(bands, 2, planes, ng, ng).transpose(2, 3, 1, 0, 4)  2.84 us
  transfers between devices with their start and end apart: 1, of which 1 were waited for; matrix products, arithmetic and copies ran while one was open for 7% of the time, Pallas kernels for 55%

commit v1 on v0

--- a/solution.py
+++ b/solution.py
@@ -114,17 +114,28 @@
     return jnp.dot(a, b, preferred_element_type=jnp.float32)
 
 
-def solve_kernel(ng, own_ref, k1_ref, k2_ref, zh_ref, zl_ref, ty_ref, sel_ref, s_ref, o_ref,
-                 buf, amp, acc, work, vec, recv, rsem, ssem, nsem, osem, orsem, lsem):
+def solve_kernel(ng, ncell, own_ref, k1_ref, k2_ref, zt_ref, ty_ref, cp_ref, s_ref, st_ref, hot_ref,
+                 o_ref, m_ref, store, amp, acc, work, vec, recv, sel, rows_buf, mine, marg,
+                 rsem, ssem, gsem, ysem, usem, dsem, wsem, osem, orsem, msem, mrsem, lsem):
     planes, _, width = own_ref.shape
+    groups = vec.shape[0]
     me = lax.axis_index("grid")
     band, nband = lax.axis_index("band"), lax.axis_size("band")
     chip, core = me // 2, me % 2
     sib = chip * 2 + (1 - core)
     cross = (1 - chip) * 2 + core
     far = (1 - chip) * 2 + (1 - core)
-    above, below = (band + 1) % nband, (band + nband - 1) % nband
+    length = nband // 2
+    side, pos = band % 2, band // 2
+    pair = band + 1 - 2 * side
+    third = (band + nband - 1 + 2 * side) % nband
+    first, last = band == 0, band == nband - 1
+    ends = jnp.logical_or(first, last)
+    wrap = jnp.where(first, nband - 1, 0)
+    has_up, has_down = pos < length - 1, pos > 0
+    up, down = jnp.where(has_up, band + 2, band), jnp.where(has_down, band - 2, band)
     mesh_id = pl.DeviceIdType.MESH
+    flat = planes * ng
 
     def remote(src, dst, send, recv_sem, device):
         return pltpu.make_async_remote_copy(
@@ -132,19 +143,63 @@
             device_id=device, device_id_type=mesh_id,
         )
 
+    def partner(blk):
+        return jnp.where(blk == 0, band, jnp.where(blk == 1, pair, third))
+
+    def place(blk, slot):
+        return jnp.where(slot == me, partner(blk), nband + blk * groups + slot)
+
     def share(blk, lane, slot, src, target):
-        return remote(src, buf.at[blk, slot], ssem.at[blk, lane], rsem.at[blk, slot], (band, target))
+        return remote(src, store.at[nband + blk * groups + slot], ssem.at[blk, lane], rsem.at[blk, slot], (band, target))
+
+    def along(block, sems, device):
+        return remote(store.at[block], store.at[block], sems.at[block], gsem.at[block], (device, me))
+
+    def came(block):
+        along(block, ysem, pair).wait_recv()
+
+    def greet(device):
+        pl.semaphore_signal(barrier, inc=1, device_id=device, device_id_type=mesh_id)
 
     barrier = pltpu.get_barrier_semaphore()
-    for device in ((band, sib), (band, cross), (band, far), (above, me), (below, me)):
-        pl.semaphore_signal(barrier, inc=1, device_id=device, device_id_type=mesh_id)
-    pl.semaphore_wait(barrier, 5)
+    for device in ((band, sib), (band, cross), (band, far), (pair, me)):
+        greet(device)
+
+    @pl.when(has_up)
+    def _():
+        greet((up, me))
+
+    @pl.when(has_down)
+    def _():
+        greet((down, me))
+
+    @pl.when(ends)
+    def _():
+        greet((wrap, me))
+
+    count = 4 + has_up.astype(jnp.int32) + has_down.astype(jnp.int32) + ends.astype(jnp.int32)
+    pl.semaphore_wait(barrier, count)
+
+    def start_own(sems, device):
+        return remote(own_ref, store.at[band], sems.at[band], gsem.at[band], (device, me))
 
     share(0, 1, me, own_ref, cross).start()
     share(0, 0, me, own_ref, sib).start()
-    remote(own_ref, buf.at[1, me], nsem.at[0], rsem.at[1, me], (above, me)).start()
-    remote(own_ref, buf.at[2, me], nsem.at[1], rsem.at[2, me], (below, me)).start()
-    local = pltpu.make_async_copy(own_ref, buf.at[0, me], lsem)
+    start_own(ysem, pair).start()
+
+    @pl.when(ends)
+    def _():
+        start_own(wsem, wrap).start()
+
+    @pl.when(has_up)
+    def _():
+        start_own(usem, up).start()
+
+    @pl.when(has_down)
+    def _():
+        start_own(dsem, down).start()
+
+    local = pltpu.make_async_copy(own_ref, store.at[band], lsem)
     local.start()
 
     def arrived(blk, slot):
@@ -152,16 +207,55 @@
 
     def relay(blk):
         arrived(blk, cross)
-        share(blk, 2, cross, buf.at[blk, cross], sib).start()
+        share(blk, 2, cross, store.at[nband + blk * groups + cross], sib).start()
 
     def spread(blk):
-        arrived(blk, me)
-        share(blk, 1, me, buf.at[blk, me], cross).start()
-        share(blk, 0, me, buf.at[blk, me], sib).start()
+        came(partner(blk))
+        share(blk, 1, me, store.at[partner(blk)], cross).start()
+        share(blk, 0, me, store.at[partner(blk)], sib).start()
+
+    def skipped(block):
+        return jnp.logical_or(
+            jnp.logical_and(pair == 0, block == nband - 1), jnp.logical_and(pair == nband - 1, block == 0)
+        )
+
+    def line(d, act):
+        lower, upper = band - 2 * d, band + 2 * d
+        has_lower, has_upper = pos - d >= 0, pos + d <= length - 1
+
+        def pass_on(block, exists, on, sems, device):
+            @pl.when(exists)
+            def _():
+                if act == "go":
+                    came(block)
+
+                @pl.when(on)
+                def _():
+                    copy = along(block, sems, device)
+                    copy.start() if act == "go" else copy.wait_send()
+
+                @pl.when(jnp.logical_not(skipped(block)))
+                def _():
+                    copy = along(block, ysem, pair)
+                    copy.start() if act == "go" else copy.wait_send()
+
+        @pl.when(side == 1)
+        def _():
+            pass_on(lower, has_lower, has_up, usem, up)
+            pass_on(upper, has_upper, has_down, dsem, down)
+
+        @pl.when(side == 0)
+        def _():
+            pass_on(upper, has_upper, has_down, dsem, down)
+            pass_on(lower, has_lower, has_up, usem, up)
 
     def ztrans(v):
         hi, lo = split(v)
-        return mm(hi, zh_ref[...]) + mm(lo, zh_ref[...]) + mm(hi, zl_ref[...])
+        parts = []
+        for h in range(2):
+            a, b = (jnp.concatenate([t[:, 128 * h:128 * h + 128], t[:, 256:]], axis=1) for t in (hi, lo))
+            parts.append(mm(a, zt_ref[h, 0]) + mm(b, zt_ref[h, 0]) + mm(a, zt_ref[h, 1]))
+        return jnp.concatenate([parts[0][:, :128], parts[1][:, :128], parts[0][:, 128:] + parts[1][:, 128:]], axis=1)
 
     def ytrans(v):
         hi, lo = split(v)
@@ -171,8 +265,17 @@
         return ((chip + s // 2) % 2) * 2 + (core + s % 2) % 2
 
     def amplitude(slot):
-        hi, lo = split(buf[0, slot].reshape(planes * ng, width))
-        amp[slot] = (mm(hi, sel_ref[me]) + mm(lo, sel_ref[me])).reshape(planes, ng, width)
+        hi, lo = split(store[place(0, slot)].reshape(flat, width))
+        parts = []
+        for h in range(2):
+            a, b = (jnp.concatenate([t[:, 128 * h:128 * h + 128], t[:, 256:]], axis=1) for t in (hi, lo))
+            parts.append(mm(a, sel[h]) + mm(b, sel[h]))
+        out = jnp.concatenate([parts[0][:, :128], parts[1][:, :128], parts[0][:, 128:] + parts[1][:, 128:]], axis=1)
+        amp[slot] = out.reshape(planes, ng, width)
+
+    for h in range(2):
+        mark = (me + 1).astype(jnp.float32)
+        sel[h] = jnp.where(cp_ref[h].astype(jnp.float32) == mark, 1.0, 0.0).astype(jnp.bfloat16)
 
     def forward(blk, s):
         slot = slot_of(s)
@@ -181,10 +284,19 @@
         def _():
             arrived(blk, sib)
 
-        @pl.when(jnp.logical_and(blk == 0, s == 2))
-        def _():
-            relay(0)
-            spread(1)
+        @pl.when(s == 2)
+        def _():
+            relay(blk)
+
+            @pl.when(blk == 0)
+            def _():
+                spread(1)
+                line(1, "go")
+
+            @pl.when(blk == 1)
+            def _():
+                spread(2)
+                line(2, "go")
 
         @pl.when(s == 3)
         def _():
@@ -194,7 +306,7 @@
         def _():
             amplitude(slot)
 
-        p = (amp[slot] * buf[blk, slot]).reshape(planes * ng, width)
+        p = (amp[slot] * store[place(blk, slot)]).reshape(flat, width)
         q = ztrans(p).reshape(planes, ng, width)
         for r in range(planes):
             work[slot, r] = ytrans(q[r])
@@ -239,7 +351,7 @@
     def inverse(blk, s):
         slot = ((chip + 1 - s // 2) % 2) * 2 + (core + s % 2 + s // 2) % 2
         q = jnp.concatenate([ytrans(work[slot, r]) for r in range(planes)], axis=0)
-        w = ztrans(q).reshape(planes, ng, width) * buf[blk, slot]
+        w = ztrans(q).reshape(planes, ng, width) * store[place(blk, slot)]
 
         @pl.when(blk == 0)
         def _():
@@ -251,7 +363,7 @@
 
         @pl.when(blk == 2)
         def _():
-            hi, lo = split((acc[slot] + w).reshape(planes * ng, width))
+            hi, lo = split((acc[slot] + w).reshape(flat, width))
             out = -(mm(hi, s_ref[...]) + mm(lo, s_ref[...]))
             vec[slot] = out.reshape(planes, ng, s_ref.shape[-1])
 
@@ -264,14 +376,6 @@
         def _():
             local.wait()
 
-        @pl.when(blk > 0)
-        def _():
-            relay(blk)
-
-        @pl.when(blk == 1)
-        def _():
-            spread(2)
-
         def fwd(s, _):
             forward(blk, s)
             return 0
@@ -285,21 +389,96 @@
             return 0
 
         lax.fori_loop(0, 4, fwd, 0)
+
+        @pl.when(blk == 2)
+        def _():
+            def more(d, _):
+                line(d, "go")
+                return 0
+
+            lax.fori_loop(3, length, more, 0)
+
         lax.fori_loop(0, ng // 16, mid, 0)
         lax.fori_loop(0, 4, inv, 0)
         return 0
 
     lax.fori_loop(0, 3, block, 0)
 
+    def settle(block, _):
+        known = jnp.logical_or(block == band, jnp.logical_or(block == pair, block == third))
+        relayed = block % 2 == side
+
+        @pl.when(jnp.logical_not(jnp.logical_or(known, relayed)))
+        def _():
+            came(block)
+
+        return 0
+
+    lax.fori_loop(0, nband, settle, 0)
+
+    def spread_out(v):
+        hi, lo = split(v.reshape(flat, v.shape[-1]))
+        return (mm(hi, st_ref[...]) + mm(lo, st_ref[...])).reshape(planes, ng, width)
+
+    def column(slot):
+        amp[0] = spread_out(o_ref[slot])
+
+        def one(block, _):
+            total = jnp.sum(store[block].reshape(flat // 8, 8, width) * amp[0].reshape(flat // 8, 8, width), axis=0)
+            rows_buf[block, slot] = total
+            return 0
+
+        lax.fori_loop(0, nband, one, 0)
+
     o_ref[me] = vec[me]
+    column(me)
     for slot in (sib, cross, far):
         remote(vec.at[slot], recv.at[slot], osem.at[slot], orsem.at[slot], (band, slot)).wait()
         o_ref[slot] = recv[slot]
+        column(slot)
+
+    lanes = jnp.sum(rows_buf[...], axis=2).reshape(groups * nband, width)
+    rest = lanes
+    terms = jnp.zeros((groups * nband, hot_ref.shape[-1]), jnp.float32)
+    for _ in range(3):
+        hi = rest.astype(jnp.bfloat16)
+        terms += mm(hi, hot_ref[...])
+        rest = rest - hi.astype(jnp.float32)
+    mine[...] = (terms / ncell).reshape(groups, nband, terms.shape[-1])
+
+    def give(slot):
+        return remote(mine.at[slot], marg.at[me], msem.at[slot], mrsem.at[me], (band, slot))
+
+    for slot in (cross, far, sib):
+        give(slot).start()
+    total = mine[me]
+    for slot in (sib, cross, far):
+        remote(mine.at[slot], marg.at[slot], msem.at[slot], mrsem.at[slot], (band, slot)).wait()
+        total += marg[slot]
+    m_ref[...] = total
+
     for blk in range(3):
         for lane, target in ((0, sib), (1, cross), (2, sib)):
             share(blk, lane, me, own_ref, target).wait_send()
-    remote(own_ref, buf.at[1, me], nsem.at[0], rsem.at[1, me], (above, me)).wait_send()
-    remote(own_ref, buf.at[2, me], nsem.at[1], rsem.at[2, me], (below, me)).wait_send()
+    start_own(ysem, pair).wait_send()
+
+    @pl.when(ends)
+    def _():
+        start_own(wsem, wrap).wait_send()
+
+    @pl.when(has_up)
+    def _():
+        start_own(usem, up).wait_send()
+
+    @pl.when(has_down)
+    def _():
+        start_own(dsem, down).wait_send()
+
+    def finish(d, _):
+        line(d, "end")
+        return 0
+
+    lax.fori_loop(1, length, finish, 0)
 
 
 def lane_tables(ng, bands):
@@ -313,38 +492,56 @@
     return half, bz // ng, bz % ng
 
 
-def solve(own, bands, groups):
+def tiles(table, half):
+    out = []
+    for h in range(2):
+        pick = np.concatenate([np.arange(128 * h, 128 * h + 128), np.arange(256, len(half))])
+        live = half[pick] == h
+        out.append(np.where(live[:, None] & live[None, :], table[pick][:, pick], 0.0))
+    return np.stack(out)
+
+
+def solve(own, bands, groups, nband):
     planes, ng, width = own.shape
     half, bnd, zed = lane_tables(ng, bands)
     ht = hartley(ng)
     th, tl = split_const(ht)
     same = (half[:, None] == half[None, :])
-    zh, zl = split_const(np.where(same & (bnd[:, None] == bnd[None, :]), ht[zed[:, None], zed[None, :]], 0.0))
+    zmat = np.where(same & (bnd[:, None] == bnd[None, :]), ht[zed[:, None], zed[None, :]], 0.0)
+    zt = np.stack(split_const(tiles(zmat, half)), axis=1)
     ty = np.concatenate([th, th, tl], axis=1)
-    copyz = same & (zed[:, None] == zed[None, :])
-    sel = np.stack([copyz & (bnd[:, None] == g) for g in range(groups)]).astype(np.float32)
+    cp = tiles(np.where(same & (zed[:, None] == zed[None, :]), bnd[:, None] + 1.0, 0.0), half)
     s = np.zeros((width, 128), np.float32)
     s[np.arange(width), half * ng + zed] = 1.0
+    hot = np.zeros((width, 128), np.float32)
+    hot[np.arange(width), bnd] = 1.0
     kv = kernel_values(ng).astype(np.float32) / np.float32(ng**3)
     kb = np.tile(kv, (1, 1, bands))
     k1 = kb[:, :, :128]
     rest = kb[:, :, 128:].reshape(kb.shape[0], ng // 16, 2, 8, 64)
     k2 = np.concatenate([rest[:, :, 0], rest[:, :, 1]], axis=-1).reshape(kb.shape[0], ng // 2, 128)
-    consts = [k1, k2, zh, zl, ty, sel.astype(jnp.bfloat16), s.astype(jnp.bfloat16)]
+    b16 = jnp.bfloat16
+    consts = [k1, k2, zt, ty, cp.astype(b16), s.astype(b16), s.T.astype(b16), hot.astype(b16)]
     full = (groups, planes, ng, width)
     f32, dma = jnp.float32, pltpu.SemaphoreType.DMA
     return pl.pallas_call(
-        functools.partial(solve_kernel, ng),
-        out_shape=jax.ShapeDtypeStruct((groups, planes, ng, 128), f32),
-        in_specs=[pl.BlockSpec(memory_space=pltpu.VMEM)] * 8,
-        out_specs=pl.BlockSpec(memory_space=pltpu.VMEM),
+        functools.partial(solve_kernel, ng, ng**3),
+        out_shape=(
+            jax.ShapeDtypeStruct((groups, planes, ng, 128), f32), jax.ShapeDtypeStruct((nband, 128), f32)
+        ),
+        in_specs=[pl.BlockSpec(memory_space=pltpu.VMEM)] * 9,
+        out_specs=(pl.BlockSpec(memory_space=pltpu.VMEM),) * 2,
         scratch_shapes=[
-            pltpu.VMEM((3,) + full, f32), pltpu.VMEM(full, f32), pltpu.VMEM(full, f32), pltpu.VMEM(full, f32),
+            pltpu.VMEM((nband + 3 * groups,) + full[1:], f32),
+            pltpu.VMEM(full, f32), pltpu.VMEM(full, f32), pltpu.VMEM(full, f32),
             pltpu.VMEM((groups, planes, ng, 128), f32), pltpu.VMEM((groups, planes, ng, 128), f32),
-            dma((3, groups)), dma((3, 3)), dma((2,)), dma((groups,)), dma((groups,)), dma(()),
+            pltpu.VMEM((2, 256, 256), b16), pltpu.VMEM((nband, groups, 8, width), f32),
+            pltpu.VMEM((groups, nband, 128), f32), pltpu.VMEM((groups, nband, 128), f32),
+            dma((3, groups)), dma((3, 3)), dma((nband,)), dma((nband,)), dma((nband,)), dma((nband,)), dma((nband,)),
+            dma((groups,)), dma((groups,)), dma((groups,)), dma((groups,)), dma(()),
         ],
         compiler_params=pltpu.CompilerParams(
-            vmem_limit_bytes=56 * 1024 * 1024, collective_id=0, has_side_effects=True
+            vmem_limit_bytes=60 * 1024 * 1024, collective_id=0, has_side_effects=True
         ),
         cost_estimate=pl.CostEstimate(flops=10**11, bytes_accessed=10**7, transcendentals=0),
         name="solve",
@@ -352,7 +549,7 @@
 
 
 def on_device(orbitals):
-    groups = lax.axis_size("grid")
+    groups, nband = lax.axis_size("grid"), lax.axis_size("band")
     bands, local = orbitals.shape
     ncell = local * groups
     ng = round(ncell ** (1 / 3))
@@ -360,20 +557,10 @@
     planes = xs // 2
     t = orbitals.reshape(bands, 2, planes, ng, ng).transpose(2, 3, 1, 0, 4).reshape(planes, ng, 2, bands * ng)
     own = jnp.concatenate([t[:, :, 0, :128], t[:, :, 1, :128], t[:, :, 0, 128:], t[:, :, 1, 128:]], axis=-1)
-    out = solve(own, bands, groups)
+    out, marg = solve(own, bands, groups, nband)
     vec = out[..., : 2 * ng].reshape(groups, planes, ng, 2, ng).transpose(0, 3, 1, 2, 4)
     vectors = vec.reshape(bands, local)
-    terms = (
-        lax.dot_general(
-            lax.all_gather(orbitals, "band", axis=0, tiled=True),
-            vectors,
-            (((1,), (1,)), ((), ())),
-            precision=lax.Precision.HIGHEST,
-            preferred_element_type=jnp.float32,
-        )
-        / ncell
-    )
-    margin = lax.psum_scatter(terms, "grid", scatter_dimension=0, tiled=True)
+    margin = marg[:, :bands].reshape(nband // groups, groups, bands).transpose(0, 2, 1).reshape(nband, groups)
     return (vectors, margin)
 
 

time: 108 us -> 75.3 us (0.70)
  between operations: 14.8 us -> 0.69 us
  waiting for transfers between devices: 13.3 us -> 0 us
  Pallas kernels: 58.7 us -> 65.3 us
  blocking collectives: 5.65 us -> 0 us
  matrix products: 3.85 us -> 0 us
  local copies, waits for them, and re-layouts: 10.3 us -> 7.63 us
    all_gather x1 -> x0, waiting for transfers between devices: 12.6 us -> none  [on_device(): lax.all_gather(orbitals, 'band', axis=0, tiled=True)]
    pallas_call x1, Pallas kernels: 58.7 us -> 65.3 us  [solve(): pl.pallas_call(functools.partial(solve_kernel, ng, ng ** 3), out_shape=(j...]
    unnamed x1 -> x0, blocking collectives: 5.65 us -> none
    unnamed x5 -> x0, local copies, waits for them, and re-layouts: 3.96 us -> none
    dot_general x1 -> x0, matrix products: 3.85 us -> none  [on_device(): lax.dot_general(lax.all_gather(orbitals, 'band', axis=0, tiled=True), vec...]
  transfers between devices with their start and end apart: 1 -> 0, of which waited for: 1 -> 0; matrix products, arithmetic and copies ran while one was open for 7% -> 0% of each run, Pallas kernels for 55% -> 0%
where the time goes in v1:
time: 75.3 us; the launch traced here: 74.5 us
  Pallas kernels  65.3 us (87%)
  local copies, waits for them, and re-layouts  7.63 us (10%)
  other arithmetic  0.87 us (1%)
    pallas_call x1, Pallas kernels, solve(): pl.pallas_call(functools.partial(solve_kernel, ng, ng ** 3), out_shape=(j...  65.3 us
    reshape x3, local copies, waits for them, and re-layouts, on_device(): orbitals.reshape(bands, 2, planes, ng, ng).transpose(2, 3, 1, 0, 4)  2.84 us
    reshape x1, local copies, waits for them, and re-layouts, on_device(): out[..., :2 * ng].reshape(groups, planes, ng, 2, ng)  1.73 us
    reshape x1, local copies, waits for them, and re-layouts, on_device(): vectors = vec.reshape(bands, local)  1.57 us

profile of v1, /device:TPU:0, one launch (start us, length us, event | category | flops | bytes accessed | tf_op | source)
XLA Modules:
  0.0 74.5 jit_solution(14746426334982117199)
XLA Ops:
  0.6 1.6 %reshape.22 = f32[4,2,6,48,48]{4,3,2,1,0:T(8,128)S(1)} reshape(f32[4,27648]{1,0:T(4,128)} %param.9) | data formatting | bytes 884736 | tf_op jit(solution)/shard_map/reshape | solution.py:558
  2.2 0.8 %copy.19 = f32[4,2,6,48,48]{4,0,3,2,1:T(4,128)S(1)} copy(f32[4,2,6,48,48]{4,3,2,1,0:T(8,128)S(1)} %reshape.22) | data formatting | bytes 884736 | tf_op jit(solution)/shard_map/reshape | solution.py:558
  3.0 0.5 reshape.23
  3.6 0.9 %pad_maximum_fusion.own_ref = f32[6,48,384]{2,1,0:T(8,128)} fusion(f32[6,48,64]{2,1,0:T(8,128)S(1)} %get-tuple-element.9, f32[6,48,64]{2,1,0:T(8,128)S(1)} %get-tuple-element.8, f32[6,48,128]{2,1,0:T(8,128)S(1)} %get-tuple-element.7, f32[6,48,128]{2,1,0:T(8,128)S(1)} %get-tuple-element.6), kind=kLoop, calls=%fused_computation.1 | loop fusion | flops 331776 | bytes 884736 | tf_op jit(solution)/shard_map/concatenate | solution.py:559
  4.4 65.3 %solve.1 = (f32[4,6,48,128]{3,2,1,0:T(8,128)}, f32[8,128]{1,0:T(8,128)}) custom-call(f32[6,48,384]{2,1,0:T(8,128)} %pad_maximum_fusion.own_ref, f32[25,48,128]{2,1,0:T(8,128)} %constant.16.clone.k1_ref, f32[25,24,128]{2,1,0:T(8,128)} %constant.17.clone.k2_ref, bf16[2,2,256,256]{3,2,1,0:T(8,128)(2,1)} %constant.18.clone.zt_ref, ...), custom_call_target="tpu_custom_call" | custom-call | flops 99999997952 | bytes 10000000 | tf_op jit(solution)/shard_map/solve/pallas_call | solution.py:527
  69.7 0.7 copy.20
  70.4 0.7 reshape.27
  71.0 1.7 %reshape.24 = f32[4,6,48,2,48]{4,3,2,1,0:T(2,128)S(1)} reshape(f32[4,6,48,96]{3,2,1,0:T(8,128)} %bitcast.29) | data formatting | bytes 884736 | tf_op jit(solution)/shard_map/reshape | solution.py:561
  72.8 0.1 copy.12
  72.9 1.6 %reshape.25 = f32[4,27648]{1,0:T(4,128)} reshape(f32[4,2,6,48,48]{4,3,2,1,0:T(8,128)S(1)} %copy.12) | data formatting | bytes 884736 | tf_op jit(solution)/shard_map/reshape | solution.py:562
  (2 shorter events, 0.0 us)

commit v2 on v1

--- a/solution.py
+++ b/solution.py
@@ -136,6 +136,7 @@
     up, down = jnp.where(has_up, band + 2, band), jnp.where(has_down, band - 2, band)
     mesh_id = pl.DeviceIdType.MESH
     flat = planes * ng
+    part = planes // 2
 
     def remote(src, dst, send, recv_sem, device):
         return pltpu.make_async_remote_copy(
@@ -149,14 +150,20 @@
     def place(blk, slot):
         return jnp.where(slot == me, partner(blk), nband + blk * groups + slot)
 
-    def share(blk, lane, slot, src, target):
-        return remote(src, store.at[nband + blk * groups + slot], ssem.at[blk, lane], rsem.at[blk, slot], (band, target))
-
-    def along(block, sems, device):
-        return remote(store.at[block], store.at[block], sems.at[block], gsem.at[block], (device, me))
-
-    def came(block):
-        along(block, ysem, pair).wait_recv()
+    def piece(ref, c):
+        return ref.at[pl.ds(c * part, part)]
+
+    def share(blk, lane, slot, src, target, c):
+        dst = store.at[nband + blk * groups + slot]
+        return remote(piece(src, c), piece(dst, c), ssem.at[blk, lane, c], rsem.at[blk, slot, c], (band, target))
+
+    def along(block, sems, device, c, src=None):
+        dst = store.at[block]
+        src = dst if src is None else src
+        return remote(piece(src, c), piece(dst, c), sems.at[block, c], gsem.at[block, c], (device, me))
+
+    def came(block, c):
+        along(block, ysem, pair, c).wait_recv()
 
     def greet(device):
         pl.semaphore_signal(barrier, inc=1, device_id=device, device_id_type=mesh_id)
@@ -180,74 +187,82 @@
     count = 4 + has_up.astype(jnp.int32) + has_down.astype(jnp.int32) + ends.astype(jnp.int32)
     pl.semaphore_wait(barrier, count)
 
-    def start_own(sems, device):
-        return remote(own_ref, store.at[band], sems.at[band], gsem.at[band], (device, me))
-
-    share(0, 1, me, own_ref, cross).start()
-    share(0, 0, me, own_ref, sib).start()
-    start_own(ysem, pair).start()
-
-    @pl.when(ends)
-    def _():
-        start_own(wsem, wrap).start()
-
-    @pl.when(has_up)
-    def _():
-        start_own(usem, up).start()
-
-    @pl.when(has_down)
-    def _():
-        start_own(dsem, down).start()
-
+    def own_copies(c, act):
+        def go(copy):
+            copy.start() if act == "go" else copy.wait_send()
+
+        go(share(0, 1, me, own_ref, cross, c))
+        go(share(0, 0, me, own_ref, sib, c))
+        go(along(band, ysem, pair, c, own_ref))
+
+        @pl.when(has_up)
+        def _():
+            go(along(band, usem, up, c, own_ref))
+
+        @pl.when(has_down)
+        def _():
+            go(along(band, dsem, down, c, own_ref))
+
+    def wrap_copies(act):
+        @pl.when(ends)
+        def _():
+            for c in range(2):
+                copy = along(band, wsem, wrap, c, own_ref)
+                copy.start() if act == "go" else copy.wait_send()
+
+    for c in range(2):
+        own_copies(c, "go")
+    wrap_copies("go")
     local = pltpu.make_async_copy(own_ref, store.at[band], lsem)
     local.start()
 
-    def arrived(blk, slot):
-        share(blk, 0, slot, own_ref, sib).wait_recv()
-
-    def relay(blk):
-        arrived(blk, cross)
-        share(blk, 2, cross, store.at[nband + blk * groups + cross], sib).start()
-
-    def spread(blk):
-        came(partner(blk))
-        share(blk, 1, me, store.at[partner(blk)], cross).start()
-        share(blk, 0, me, store.at[partner(blk)], sib).start()
+    def arrived(blk, slot, c):
+        share(blk, 0, slot, own_ref, sib, c).wait_recv()
+
+    def relay(blk, c):
+        arrived(blk, cross, c)
+        share(blk, 2, cross, store.at[nband + blk * groups + cross], sib, c).start()
+
+    def spread(blk, c):
+        came(partner(blk), c)
+        share(blk, 1, me, store.at[partner(blk)], cross, c).start()
+        share(blk, 0, me, store.at[partner(blk)], sib, c).start()
 
     def skipped(block):
         return jnp.logical_or(
             jnp.logical_and(pair == 0, block == nband - 1), jnp.logical_and(pair == nband - 1, block == 0)
         )
 
-    def line(d, act):
-        lower, upper = band - 2 * d, band + 2 * d
-        has_lower, has_upper = pos - d >= 0, pos + d <= length - 1
-
+    def line(d, c, near, act):
         def pass_on(block, exists, on, sems, device):
             @pl.when(exists)
             def _():
                 if act == "go":
-                    came(block)
+                    came(block, c)
+
+                def one(copy):
+                    copy.start() if act == "go" else copy.wait_send()
+
+                @pl.when(jnp.logical_not(skipped(block)))
+                def _():
+                    one(along(block, ysem, pair, c))
 
                 @pl.when(on)
                 def _():
-                    copy = along(block, sems, device)
-                    copy.start() if act == "go" else copy.wait_send()
-
-                @pl.when(jnp.logical_not(skipped(block)))
-                def _():
-                    copy = along(block, ysem, pair)
-                    copy.start() if act == "go" else copy.wait_send()
-
-        @pl.when(side == 1)
-        def _():
-            pass_on(lower, has_lower, has_up, usem, up)
-            pass_on(upper, has_upper, has_down, dsem, down)
-
-        @pl.when(side == 0)
-        def _():
-            pass_on(upper, has_upper, has_down, dsem, down)
-            pass_on(lower, has_lower, has_up, usem, up)
+                    one(along(block, sems, device, c))
+
+        upward = (side == 1) == near
+        pass_on(band - 2 * d, jnp.logical_and(upward, pos - d >= 0), has_up, usem, up)
+        pass_on(
+            band + 2 * d, jnp.logical_and(jnp.logical_not(upward), pos + d <= length - 1), has_down, dsem, down
+        )
+
+    def serve(blk, c):
+        @pl.when(blk < 2)
+        def _():
+            spread(blk + 1, c)
+
+        line(blk + 1, c, True, "go")
 
     def ztrans(v):
         hi, lo = split(v)
@@ -261,55 +276,52 @@
         hi, lo = split(v)
         return mm(ty_ref[...], jnp.concatenate([hi, lo, hi], axis=0))
 
-    def slot_of(s):
-        return ((chip + s // 2) % 2) * 2 + (core + s % 2) % 2
-
-    def amplitude(slot):
-        hi, lo = split(store[place(0, slot)].reshape(flat, width))
+    def amplitude(slot, rows):
+        hi, lo = split(store[place(0, slot), rows].reshape(part * ng, width))
         parts = []
         for h in range(2):
             a, b = (jnp.concatenate([t[:, 128 * h:128 * h + 128], t[:, 256:]], axis=1) for t in (hi, lo))
             parts.append(mm(a, sel[h]) + mm(b, sel[h]))
         out = jnp.concatenate([parts[0][:, :128], parts[1][:, :128], parts[0][:, 128:] + parts[1][:, 128:]], axis=1)
-        amp[slot] = out.reshape(planes, ng, width)
+        amp[slot, rows] = out.reshape(part, ng, width)
 
     for h in range(2):
         mark = (me + 1).astype(jnp.float32)
         sel[h] = jnp.where(cp_ref[h].astype(jnp.float32) == mark, 1.0, 0.0).astype(jnp.bfloat16)
 
-    def forward(blk, s):
-        slot = slot_of(s)
-
-        @pl.when(s == 1)
-        def _():
-            arrived(blk, sib)
-
-        @pl.when(s == 2)
-        def _():
-            relay(blk)
-
-            @pl.when(blk == 0)
+    def forward(blk, i):
+        slot = ((chip + i // 4) % 2) * 2 + (core + i % 2) % 2
+        c = (i // 2) % 2
+        rows = pl.ds(c * part, part)
+
+        @pl.when(jnp.logical_or(i == 1, i == 3))
+        def _():
+            arrived(blk, sib, c)
+
+        @pl.when(jnp.logical_or(i == 4, i == 6))
+        def _():
+            @pl.when(jnp.logical_or(blk == 0, i == 6))
             def _():
-                spread(1)
-                line(1, "go")
-
-            @pl.when(blk == 1)
+                serve(blk, c)
+
+            relay(blk, c)
+
+            @pl.when(jnp.logical_and(blk > 0, i == 6))
             def _():
-                spread(2)
-                line(2, "go")
-
-        @pl.when(s == 3)
-        def _():
-            arrived(blk, far)
+                line(blk, c, False, "go")
+
+        @pl.when(jnp.logical_or(i == 5, i == 7))
+        def _():
+            arrived(blk, far, c)
 
         @pl.when(blk == 0)
         def _():
-            amplitude(slot)
-
-        p = (amp[slot] * store[place(blk, slot)]).reshape(flat, width)
-        q = ztrans(p).reshape(planes, ng, width)
-        for r in range(planes):
-            work[slot, r] = ytrans(q[r])
+            amplitude(slot, rows)
+
+        p = (amp[slot, rows] * store[place(blk, slot), rows]).reshape(part * ng, width)
+        q = ztrans(p).reshape(part, ng, width)
+        for r in range(part):
+            work[slot, c * part + r] = ytrans(q[r])
 
     def conv(vals, kern):
         spec = rfft(vals)
@@ -353,6 +365,11 @@
         q = jnp.concatenate([ytrans(work[slot, r]) for r in range(planes)], axis=0)
         w = ztrans(q).reshape(planes, ng, width) * store[place(blk, slot)]
 
+        @pl.when(jnp.logical_and(blk < 2, s == 2))
+        def _():
+            serve(blk + 1, 0)
+            line(blk + 1, 0, False, "go")
+
         @pl.when(blk == 0)
         def _():
             acc[slot] = w
@@ -376,8 +393,8 @@
         def _():
             local.wait()
 
-        def fwd(s, _):
-            forward(blk, s)
+        def fwd(i, _):
+            forward(blk, i)
             return 0
 
         def mid(t, _):
@@ -388,29 +405,29 @@
             inverse(blk, s)
             return 0
 
-        lax.fori_loop(0, 4, fwd, 0)
-
-        @pl.when(blk == 2)
-        def _():
-            def more(d, _):
-                line(d, "go")
-                return 0
-
-            lax.fori_loop(3, length, more, 0)
-
+        lax.fori_loop(0, 8, fwd, 0)
         lax.fori_loop(0, ng // 16, mid, 0)
         lax.fori_loop(0, 4, inv, 0)
         return 0
 
     lax.fori_loop(0, 3, block, 0)
 
+    def later(d, _):
+        for c in range(2):
+            line(d, c, False, "go")
+            line(d + 1, c, True, "go")
+        return 0
+
+    lax.fori_loop(3, length, later, 0)
+
     def settle(block, _):
         known = jnp.logical_or(block == band, jnp.logical_or(block == pair, block == third))
         relayed = block % 2 == side
 
         @pl.when(jnp.logical_not(jnp.logical_or(known, relayed)))
         def _():
-            came(block)
+            for c in range(2):
+                came(block, c)
 
         return 0
 
@@ -457,28 +474,28 @@
         total += marg[slot]
     m_ref[...] = total
 
-    for blk in range(3):
-        for lane, target in ((0, sib), (1, cross), (2, sib)):
-            share(blk, lane, me, own_ref, target).wait_send()
-    start_own(ysem, pair).wait_send()
-
-    @pl.when(ends)
-    def _():
-        start_own(wsem, wrap).wait_send()
-
-    @pl.when(has_up)
-    def _():
-        start_own(usem, up).wait_send()
-
-    @pl.when(has_down)
-    def _():
-        start_own(dsem, down).wait_send()
-
-    def finish(d, _):
-        line(d, "end")
+    wrap_copies("end")
+    for c in range(2):
+        own_copies(c, "end")
+
+    def finish(i, _):
+        blk, c = 1 + i // 2, i % 2
+        for lane, target in ((0, sib), (1, cross)):
+            share(blk, lane, me, own_ref, target, c).wait_send()
         return 0
 
-    lax.fori_loop(1, length, finish, 0)
+    def finish_relay(i, _):
+        share(i // 2, 2, me, own_ref, sib, i % 2).wait_send()
+        return 0
+
+    def finish_line(i, _):
+        line(1 + i // 2, i % 2, True, "end")
+        line(1 + i // 2, i % 2, False, "end")
+        return 0
+
+    lax.fori_loop(0, 4, finish, 0)
+    lax.fori_loop(0, 6, finish_relay, 0)
+    lax.fori_loop(0, 2 * (length - 1), finish_line, 0)
 
 
 def lane_tables(ng, bands):
@@ -537,7 +554,8 @@
             pltpu.VMEM((groups, planes, ng, 128), f32), pltpu.VMEM((groups, planes, ng, 128), f32),
             pltpu.VMEM((2, 256, 256), b16), pltpu.VMEM((nband, groups, 8, width), f32),
             pltpu.VMEM((groups, nband, 128), f32), pltpu.VMEM((groups, nband, 128), f32),
-            dma((3, groups)), dma((3, 3)), dma((nband,)), dma((nband,)), dma((nband,)), dma((nband,)), dma((nband,)),
+            dma((3, groups, 2)), dma((3, 3, 2)), dma((nband, 2)), dma((nband, 2)), dma((nband, 2)), dma((nband, 2)),
+            dma((nband, 2)),
             dma((groups,)), dma((groups,)), dma((groups,)), dma((groups,)), dma(()),
         ],
         compiler_params=pltpu.CompilerParams(

time: 75.3 us -> 68.6 us (0.911)
  Pallas kernels: 65.3 us -> 59.1 us
    pallas_call x1, Pallas kernels: 65.3 us -> 59.1 us  [solve(): pl.pallas_call(functools.partial(solve_kernel, ng, ng ** 3), out_shape=(j...]
where the time goes in v2:
time: 68.6 us; the launch traced here: 68.3 us
  Pallas kernels  59.1 us (86%)
  local copies, waits for them, and re-layouts  7.63 us (11%)
  other arithmetic  0.87 us (1%)
  between operations  0.69 us (1%)
    pallas_call x1, Pallas kernels, solve(): pl.pallas_call(functools.partial(solve_kernel, ng, ng ** 3), out_shape=(j...  59.1 us
    reshape x3, local copies, waits for them, and re-layouts, on_device(): orbitals.reshape(bands, 2, planes, ng, ng).transpose(2, 3, 1, 0, 4)  2.84 us
    reshape x1, local copies, waits for them, and re-layouts, on_device(): out[..., :2 * ng].reshape(groups, planes, ng, 2, ng)  1.73 us
    reshape x1, local copies, waits for them, and re-layouts, on_device(): vectors = vec.reshape(bands, local)  1.57 us

profile of v2, /device:TPU:0, one launch (start us, length us, event | category | flops | bytes accessed | tf_op | source)
XLA Modules:
  0.0 68.3 jit_solution(103271707428545229)
XLA Ops:
  0.6 1.6 %reshape.22 = f32[4,2,6,48,48]{4,3,2,1,0:T(8,128)S(1)} reshape(f32[4,27648]{1,0:T(4,128)} %param.9) | data formatting | bytes 884736 | tf_op jit(solution)/shard_map/reshape | solution.py:576
  2.2 0.8 %copy.19 = f32[4,2,6,48,48]{4,0,3,2,1:T(4,128)S(1)} copy(f32[4,2,6,48,48]{4,3,2,1,0:T(8,128)S(1)} %reshape.22) | data formatting | bytes 884736 | tf_op jit(solution)/shard_map/reshape | solution.py:576
  3.0 0.5 reshape.23
  3.6 0.9 %pad_maximum_fusion.own_ref = f32[6,48,384]{2,1,0:T(8,128)} fusion(f32[6,48,64]{2,1,0:T(8,128)S(1)} %get-tuple-element.9, f32[6,48,64]{2,1,0:T(8,128)S(1)} %get-tuple-element.8, f32[6,48,128]{2,1,0:T(8,128)S(1)} %get-tuple-element.7, f32[6,48,128]{2,1,0:T(8,128)S(1)} %get-tuple-element.6), kind=kLoop, calls=%fused_computation.1 | loop fusion | flops 331776 | bytes 884736 | tf_op jit(solution)/shard_map/concatenate | solution.py:577
  4.4 59.1 %solve.1 = (f32[4,6,48,128]{3,2,1,0:T(8,128)}, f32[8,128]{1,0:T(8,128)}) custom-call(f32[6,48,384]{2,1,0:T(8,128)} %pad_maximum_fusion.own_ref, f32[25,48,128]{2,1,0:T(8,128)} %constant.16.clone.k1_ref, f32[25,24,128]{2,1,0:T(8,128)} %constant.17.clone.k2_ref, bf16[2,2,256,256]{3,2,1,0:T(8,128)(2,1)} %constant.18.clone.zt_ref, ...), custom_call_target="tpu_custom_call" | custom-call | flops 99999997952 | bytes 10000000 | tf_op jit(solution)/shard_map/solve/pallas_call | solution.py:544
  63.6 0.7 copy.20
  64.2 0.7 reshape.27
  64.9 1.7 %reshape.24 = f32[4,6,48,2,48]{4,3,2,1,0:T(2,128)S(1)} reshape(f32[4,6,48,96]{3,2,1,0:T(8,128)} %bitcast.29) | data formatting | bytes 884736 | tf_op jit(solution)/shard_map/reshape | solution.py:579
  66.7 0.1 copy.12
  66.8 1.6 %reshape.25 = f32[4,27648]{1,0:T(4,128)} reshape(f32[4,2,6,48,48]{4,3,2,1,0:T(8,128)S(1)} %copy.12) | data formatting | bytes 884736 | tf_op jit(solution)/shard_map/reshape | solution.py:580
  (2 shorter events, 0.0 us)

commit v3 on v2

--- a/solution.py
+++ b/solution.py
@@ -114,10 +114,17 @@
     return jnp.dot(a, b, preferred_element_type=jnp.float32)
 
 
-def solve_kernel(ng, ncell, own_ref, k1_ref, k2_ref, zt_ref, ty_ref, cp_ref, s_ref, st_ref, hot_ref,
-                 o_ref, m_ref, store, amp, acc, work, vec, recv, sel, rows_buf, mine, marg,
-                 rsem, ssem, gsem, ysem, usem, dsem, wsem, osem, orsem, msem, mrsem, lsem):
-    planes, _, width = own_ref.shape
+def solve_kernel(ng, ncell, nat_ref, *refs):
+    tables, refs = refs[:7], refs[7:]
+    (o_ref, m_ref, k1_ref, k2_ref, zt_ref, ty_ref, cp_ref, s_ref, hot_ref, own_ref, store, amp, acc, work, vec, recv, sel,
+     rows_buf, mine, marg, rsem, ssem, gsem, ysem, usem, dsem, wsem, osem, orsem, msem, mrsem, lsem, csem, esem, tmp, ebuf) = refs
+    kept = (k1_ref, k2_ref, zt_ref, ty_ref, cp_ref, s_ref, hot_ref)
+    loads = [pltpu.make_async_copy(src, dst, csem.at[n]) for n, (src, dst) in enumerate(zip(tables, kept))]
+    for n in (4, 2, 3, 0, 1, 5, 6):
+        loads[n].start()
+    bands = nat_ref.shape[0]
+    flat, width = own_ref.shape
+    planes = flat // ng
     groups = vec.shape[0]
     me = lax.axis_index("grid")
     band, nband = lax.axis_index("band"), lax.axis_size("band")
@@ -135,7 +142,6 @@
     has_up, has_down = pos < length - 1, pos > 0
     up, down = jnp.where(has_up, band + 2, band), jnp.where(has_down, band - 2, band)
     mesh_id = pl.DeviceIdType.MESH
-    flat = planes * ng
     part = planes // 2
 
     def remote(src, dst, send, recv_sem, device):
@@ -151,7 +157,7 @@
         return jnp.where(slot == me, partner(blk), nband + blk * groups + slot)
 
     def piece(ref, c):
-        return ref.at[pl.ds(c * part, part)]
+        return ref.at[pl.ds(c * part * ng, part * ng)]
 
     def share(blk, lane, slot, src, target, c):
         dst = store.at[nband + blk * groups + slot]
@@ -165,6 +171,55 @@
     def came(block, c):
         along(block, ysem, pair, c).wait_recv()
 
+    lane = lax.broadcasted_iota(jnp.int32, (1, 128), 1)
+
+    def moved(value, shift, low, high, under):
+        out = pltpu.roll(value, shift % 128, 1) if shift % 128 else value
+        return jnp.where(jnp.logical_and(lane >= low, lane < high), out, under)
+
+    def gather_in(read, want, blank):
+        for y0 in range(8):
+            chunks = [None, None, None]
+            for h in range(2):
+                for b in range(bands):
+                    for target, start, stop, base in ((h, 0, 128, 0), (2, 128, bands * ng, 64 * h)):
+                        first, final = max(start, b * ng), min(stop, b * ng + ng)
+                        if first >= final:
+                            continue
+                        source = y0 * ng + first - b * ng
+                        place_at = first - start + base
+                        while first < final:
+                            q, off = source // 128, source % 128
+                            size = min(final - first, 128 - off)
+                            under = chunks[target]
+                            under = blank if under is None else under
+                            chunks[target] = moved(read(b, h, q), place_at - off, place_at, place_at + size, under)
+                            first, source, place_at = first + size, source + size, place_at + size
+            for j, value in enumerate(chunks):
+                want(j, y0, value)
+
+    def scatter_out(read, write, blank):
+        for h in range(2):
+            chunks = [blank] * 3
+            for y0 in range(8):
+                value = read(y0)
+                source, at, left = h * ng, y0 * ng, ng
+                while left > 0:
+                    q, off = at // 128, at % 128
+                    size = min(left, 128 - off)
+                    chunks[q] = moved(value, off - source, off, off + size, chunks[q])
+                    source, at, left = source + size, at + size, left - size
+            for q in range(3):
+                write(h, q, chunks[q])
+
+    group = flat // 8
+
+    def packed(h, q):
+        return pl.ds(q + 3 * group * h, group, stride=3)
+
+    def spaced(y0):
+        return pl.ds(y0, group, stride=8)
+
     def greet(device):
         pl.semaphore_signal(barrier, inc=1, device_id=device, device_id_type=mesh_id)
 
@@ -185,8 +240,6 @@
         greet((wrap, me))
 
     count = 4 + has_up.astype(jnp.int32) + has_down.astype(jnp.int32) + ends.astype(jnp.int32)
-    pl.semaphore_wait(barrier, count)
-
     def own_copies(c, act):
         def go(copy):
             copy.start() if act == "go" else copy.wait_send()
@@ -210,6 +263,12 @@
                 copy = along(band, wsem, wrap, c, own_ref)
                 copy.start() if act == "go" else copy.wait_send()
 
+    def put_own(j, y0, value):
+        ebuf[0, j, spaced(y0), :] = value
+
+    gather_in(lambda b, h, q: nat_ref[b, packed(h, q), :], put_own, jnp.zeros((group, 128), jnp.float32))
+    own_ref[...] = jnp.concatenate([ebuf[0, j] for j in range(3)], axis=1)
+    pl.semaphore_wait(barrier, count)
     for c in range(2):
         own_copies(c, "go")
     wrap_copies("go")
@@ -276,52 +335,67 @@
         hi, lo = split(v)
         return mm(ty_ref[...], jnp.concatenate([hi, lo, hi], axis=0))
 
-    def amplitude(slot, rows):
-        hi, lo = split(store[place(0, slot), rows].reshape(part * ng, width))
+    def amplitude(v):
+        hi, lo = split(v)
         parts = []
         for h in range(2):
             a, b = (jnp.concatenate([t[:, 128 * h:128 * h + 128], t[:, 256:]], axis=1) for t in (hi, lo))
             parts.append(mm(a, sel[h]) + mm(b, sel[h]))
-        out = jnp.concatenate([parts[0][:, :128], parts[1][:, :128], parts[0][:, 128:] + parts[1][:, 128:]], axis=1)
-        amp[slot, rows] = out.reshape(part, ng, width)
-
+        return jnp.concatenate([parts[0][:, :128], parts[1][:, :128], parts[0][:, 128:] + parts[1][:, 128:]], axis=1)
+
+    for n in (4, 2, 3):
+        loads[n].wait()
     for h in range(2):
         mark = (me + 1).astype(jnp.float32)
         sel[h] = jnp.where(cp_ref[h].astype(jnp.float32) == mark, 1.0, 0.0).astype(jnp.bfloat16)
 
-    def forward(blk, i):
-        slot = ((chip + i // 4) % 2) * 2 + (core + i % 2) % 2
-        c = (i // 2) % 2
-        rows = pl.ds(c * part, part)
-
-        @pl.when(jnp.logical_or(i == 1, i == 3))
-        def _():
-            arrived(blk, sib, c)
-
-        @pl.when(jnp.logical_or(i == 4, i == 6))
-        def _():
-            @pl.when(jnp.logical_or(blk == 0, i == 6))
-            def _():
-                serve(blk, c)
-
-            relay(blk, c)
-
-            @pl.when(jnp.logical_and(blk > 0, i == 6))
-            def _():
-                line(blk, c, False, "go")
-
-        @pl.when(jnp.logical_or(i == 5, i == 7))
+    def transform(blk, slots, c):
+        rows = pl.ds(c * part * ng, part * ng)
+
+        @pl.when(blk == 0)
+        def _():
+            own = jnp.concatenate([store[place(0, slot), rows] for slot in slots], axis=0)
+            out = amplitude(own).reshape(len(slots), part * ng, width)
+            for n, slot in enumerate(slots):
+                amp[slot, rows] = out[n]
+
+        p = jnp.concatenate([amp[slot, rows] * store[place(blk, slot), rows] for slot in slots], axis=0)
+        q = ztrans(p).reshape(len(slots), part, ng, width)
+        for n, slot in enumerate(slots):
+            for r in range(part):
+                work[slot, c * part + r] = ytrans(q[n, r])
+
+    def near(blk, c):
+        arrived(blk, sib, c)
+
+        @pl.when(jnp.logical_and(blk > 0, c == 1))
+        def _():
+            relay(blk, 0)
+
+        transform(blk, (me, sib), c)
+
+    def other(blk, i):
+        c = i // 2
+
+        @pl.when(jnp.logical_and(blk == 0, i == 0))
+        def _():
+            serve(blk, 0)
+            relay(blk, 0)
+
+        @pl.when(i == 1)
+        def _():
+            serve(blk, 1)
+            relay(blk, 1)
+
+        @pl.when(i % 2 == 1)
         def _():
             arrived(blk, far, c)
 
-        @pl.when(blk == 0)
-        def _():
-            amplitude(slot, rows)
-
-        p = (amp[slot, rows] * store[place(blk, slot), rows]).reshape(part * ng, width)
-        q = ztrans(p).reshape(part, ng, width)
-        for r in range(part):
-            work[slot, c * part + r] = ytrans(q[r])
+        @pl.when(jnp.logical_and(blk > 0, i == 2))
+        def _():
+            line(blk, 1, False, "go")
+
+        transform(blk, (jnp.where(i % 2 == 0, cross, far),), c)
 
     def conv(vals, kern):
         spec = rfft(vals)
@@ -363,7 +437,7 @@
     def inverse(blk, s):
         slot = ((chip + 1 - s // 2) % 2) * 2 + (core + s % 2 + s // 2) % 2
         q = jnp.concatenate([ytrans(work[slot, r]) for r in range(planes)], axis=0)
-        w = ztrans(q).reshape(planes, ng, width) * store[place(blk, slot)]
+        w = ztrans(q) * store[place(blk, slot)]
 
         @pl.when(jnp.logical_and(blk < 2, s == 2))
         def _():
@@ -380,9 +454,13 @@
 
         @pl.when(blk == 2)
         def _():
-            hi, lo = split((acc[slot] + w).reshape(flat, width))
-            out = -(mm(hi, s_ref[...]) + mm(lo, s_ref[...]))
-            vec[slot] = out.reshape(planes, ng, s_ref.shape[-1])
+            hi, lo = split(acc[slot] + w)
+            tmp[...] = -(mm(hi, s_ref[...]) + mm(lo, s_ref[...]))
+
+            def put_vec(h, q, value):
+                vec[slot, packed(h, q), :] = value
+
+            scatter_out(lambda y0: tmp[spaced(y0), :], put_vec, jnp.zeros((group, 128), jnp.float32))
 
             @pl.when(s < 3)
             def _():
@@ -393,8 +471,12 @@
         def _():
             local.wait()
 
-        def fwd(i, _):
-            forward(blk, i)
+        def fwd_near(c, _):
+            near(blk, c)
+            return 0
+
+        def fwd_other(i, _):
+            other(blk, i)
             return 0
 
         def mid(t, _):
@@ -405,7 +487,14 @@
             inverse(blk, s)
             return 0
 
-        lax.fori_loop(0, 8, fwd, 0)
+        lax.fori_loop(0, 2, fwd_near, 0)
+        lax.fori_loop(0, 4, fwd_other, 0)
+
+        @pl.when(blk == 0)
+        def _():
+            for n in (0, 1, 5, 6):
+                loads[n].wait()
+
         lax.fori_loop(0, ng // 16, mid, 0)
         lax.fori_loop(0, 4, inv, 0)
         return 0
@@ -420,47 +509,72 @@
 
     lax.fori_loop(3, length, later, 0)
 
-    def settle(block, _):
-        known = jnp.logical_or(block == band, jnp.logical_or(block == pair, block == third))
-        relayed = block % 2 == side
-
-        @pl.when(jnp.logical_not(jnp.logical_or(known, relayed)))
+    def emit(src, slot):
+        return pltpu.make_async_copy(src.at[slot], o_ref.at[slot], esem.at[slot])
+
+    def spread_out(src, slot, n):
+        def put(j, y0, value):
+            ebuf[n, j, spaced(y0), :] = value
+
+        gather_in(lambda b, h, q: src[slot, packed(h, q), :], put, jnp.zeros((group, 128), jnp.float32))
+
+    def columns(block, slots):
+        parts = [[jnp.zeros((8, 128), jnp.float32) for _ in range(3)] for _ in slots]
+        for r in range(flat // 8):
+            for j in range(3):
+                phi = store[block, pl.ds(8 * r, 8), pl.ds(128 * j, 128)]
+                for n, p in enumerate(parts):
+                    p[j] = p[j] + phi * ebuf[n, j, pl.ds(8 * r, 8)]
+        for slot, p in zip(slots, parts):
+            rows_buf[block, slot] = jnp.concatenate(p, axis=1)
+
+    def ready(block):
+        near_by = jnp.logical_or(block == pair, block == third)
+        return jnp.logical_or(near_by, block % 2 == side)
+
+    def early(block, _):
+        @pl.when(ready(block))
+        def _():
+            columns(block, (me, sib))
+
+        return 0
+
+    def late(block, _):
+        @pl.when(jnp.logical_not(ready(block)))
         def _():
             for c in range(2):
                 came(block, c)
+            columns(block, (me, sib))
 
         return 0
 
-    lax.fori_loop(0, nband, settle, 0)
-
-    def spread_out(v):
-        hi, lo = split(v.reshape(flat, v.shape[-1]))
-        return (mm(hi, st_ref[...]) + mm(lo, st_ref[...])).reshape(planes, ng, width)
-
-    def column(slot):
-        amp[0] = spread_out(o_ref[slot])
-
-        def one(block, _):
-            total = jnp.sum(store[block].reshape(flat // 8, 8, width) * amp[0].reshape(flat // 8, 8, width), axis=0)
-            rows_buf[block, slot] = total
-            return 0
-
-        lax.fori_loop(0, nband, one, 0)
-
-    o_ref[me] = vec[me]
-    column(me)
-    for slot in (sib, cross, far):
+    def rest(block, _):
+        columns(block, (cross, far))
+        return 0
+
+    def settle(slot):
         remote(vec.at[slot], recv.at[slot], osem.at[slot], orsem.at[slot], (band, slot)).wait()
-        o_ref[slot] = recv[slot]
-        column(slot)
+        emit(recv, slot).start()
+
+    emit(vec, me).start()
+    spread_out(vec, me, 0)
+    settle(sib)
+    spread_out(recv, sib, 1)
+    lax.fori_loop(0, nband, early, 0)
+    lax.fori_loop(0, nband, late, 0)
+    settle(cross)
+    spread_out(recv, cross, 0)
+    settle(far)
+    spread_out(recv, far, 1)
+    lax.fori_loop(0, nband, rest, 0)
 
     lanes = jnp.sum(rows_buf[...], axis=2).reshape(groups * nband, width)
-    rest = lanes
+    left_over = lanes
     terms = jnp.zeros((groups * nband, hot_ref.shape[-1]), jnp.float32)
     for _ in range(3):
-        hi = rest.astype(jnp.bfloat16)
+        hi = left_over.astype(jnp.bfloat16)
         terms += mm(hi, hot_ref[...])
-        rest = rest - hi.astype(jnp.float32)
+        left_over = left_over - hi.astype(jnp.float32)
     mine[...] = (terms / ncell).reshape(groups, nband, terms.shape[-1])
 
     def give(slot):
@@ -468,34 +582,35 @@
 
     for slot in (cross, far, sib):
         give(slot).start()
+    for slot in range(groups):
+        emit(recv, slot).wait()
+    wrap_copies("end")
+    for c in range(2):
+        own_copies(c, "end")
+
+    def finish(i, _):
+        blk, c = 1 + i // 2, i % 2
+        for lane, target in ((0, sib), (1, cross)):
+            share(blk, lane, me, own_ref, target, c).wait_send()
+        return 0
+
+    def finish_relay(i, _):
+        share(i // 2, 2, me, own_ref, sib, i % 2).wait_send()
+        return 0
+
+    def finish_line(i, _):
+        line(1 + i // 2, i % 2, True, "end")
+        line(1 + i // 2, i % 2, False, "end")
+        return 0
+
+    lax.fori_loop(0, 4, finish, 0)
+    lax.fori_loop(0, 6, finish_relay, 0)
+    lax.fori_loop(0, 2 * (length - 1), finish_line, 0)
     total = mine[me]
     for slot in (sib, cross, far):
         remote(mine.at[slot], marg.at[slot], msem.at[slot], mrsem.at[slot], (band, slot)).wait()
         total += marg[slot]
     m_ref[...] = total
-
-    wrap_copies("end")
-    for c in range(2):
-        own_copies(c, "end")
-
-    def finish(i, _):
-        blk, c = 1 + i // 2, i % 2
-        for lane, target in ((0, sib), (1, cross)):
-            share(blk, lane, me, own_ref, target, c).wait_send()
-        return 0
-
-    def finish_relay(i, _):
-        share(i // 2, 2, me, own_ref, sib, i % 2).wait_send()
-        return 0
-
-    def finish_line(i, _):
-        line(1 + i // 2, i % 2, True, "end")
-        line(1 + i // 2, i % 2, False, "end")
-        return 0
-
-    lax.fori_loop(0, 4, finish, 0)
-    lax.fori_loop(0, 6, finish_relay, 0)
-    lax.fori_loop(0, 2 * (length - 1), finish_line, 0)
 
 
 def lane_tables(ng, bands):
@@ -518,8 +633,10 @@
     return np.stack(out)
 
 
-def solve(own, bands, groups, nband):
-    planes, ng, width = own.shape
+def solve(nat, ng, groups, nband):
+    bands = nat.shape[0]
+    width = 2 * bands * ng
+    flat = nat.shape[1] * nat.shape[2] // (2 * ng)
     half, bnd, zed = lane_tables(ng, bands)
     ht = hartley(ng)
     th, tl = split_const(ht)
@@ -538,32 +655,35 @@
     rest = kb[:, :, 128:].reshape(kb.shape[0], ng // 16, 2, 8, 64)
     k2 = np.concatenate([rest[:, :, 0], rest[:, :, 1]], axis=-1).reshape(kb.shape[0], ng // 2, 128)
     b16 = jnp.bfloat16
-    consts = [k1, k2, zt, ty, cp.astype(b16), s.astype(b16), s.T.astype(b16), hot.astype(b16)]
-    full = (groups, planes, ng, width)
+    consts = [k1, k2, zt, ty, cp.astype(b16), s.astype(b16), hot.astype(b16)]
+    full = (groups, flat, width)
+    slim = (groups,) + nat.shape[1:]
     f32, dma = jnp.float32, pltpu.SemaphoreType.DMA
     return pl.pallas_call(
         functools.partial(solve_kernel, ng, ng**3),
         out_shape=(
-            jax.ShapeDtypeStruct((groups, planes, ng, 128), f32), jax.ShapeDtypeStruct((nband, 128), f32)
+            jax.ShapeDtypeStruct(slim, f32), jax.ShapeDtypeStruct((nband, 128), f32)
         ),
-        in_specs=[pl.BlockSpec(memory_space=pltpu.VMEM)] * 9,
-        out_specs=(pl.BlockSpec(memory_space=pltpu.VMEM),) * 2,
+        in_specs=[pl.BlockSpec(memory_space=pltpu.VMEM)] + [pl.BlockSpec(memory_space=pl.ANY)] * len(consts),
+        out_specs=(pl.BlockSpec(memory_space=pl.ANY), pl.BlockSpec(memory_space=pltpu.VMEM)),
         scratch_shapes=[
-            pltpu.VMEM((nband + 3 * groups,) + full[1:], f32),
-            pltpu.VMEM(full, f32), pltpu.VMEM(full, f32), pltpu.VMEM(full, f32),
-            pltpu.VMEM((groups, planes, ng, 128), f32), pltpu.VMEM((groups, planes, ng, 128), f32),
+            *[pltpu.VMEM(c.shape, c.dtype) for c in consts],
+            pltpu.VMEM(full[1:], f32), pltpu.VMEM((nband + 3 * groups,) + full[1:], f32),
+            pltpu.VMEM(full, f32), pltpu.VMEM(full, f32), pltpu.VMEM((groups, flat // ng, ng, width), f32),
+            pltpu.VMEM(slim, f32), pltpu.VMEM(slim, f32),
             pltpu.VMEM((2, 256, 256), b16), pltpu.VMEM((nband, groups, 8, width), f32),
             pltpu.VMEM((groups, nband, 128), f32), pltpu.VMEM((groups, nband, 128), f32),
             dma((3, groups, 2)), dma((3, 3, 2)), dma((nband, 2)), dma((nband, 2)), dma((nband, 2)), dma((nband, 2)),
             dma((nband, 2)),
-            dma((groups,)), dma((groups,)), dma((groups,)), dma((groups,)), dma(()),
+            dma((groups,)), dma((groups,)), dma((groups,)), dma((groups,)), dma(()), dma((len(consts),)), dma((groups,)),
+            pltpu.VMEM((flat, 128), f32), pltpu.VMEM((2, 3, flat, 128), f32),
         ],
         compiler_params=pltpu.CompilerParams(
             vmem_limit_bytes=60 * 1024 * 1024, collective_id=0, has_side_effects=True
         ),
         cost_estimate=pl.CostEstimate(flops=10**11, bytes_accessed=10**7, transcendentals=0),
         name="solve",
-    )(own, *[jnp.asarray(c) for c in consts])
+    )(nat, *[jnp.asarray(c) for c in consts])
 
 
 def on_device(orbitals):
@@ -571,13 +691,8 @@
     bands, local = orbitals.shape
     ncell = local * groups
     ng = round(ncell ** (1 / 3))
-    xs = local // (ng * ng)
-    planes = xs // 2
-    t = orbitals.reshape(bands, 2, planes, ng, ng).transpose(2, 3, 1, 0, 4).reshape(planes, ng, 2, bands * ng)
-    own = jnp.concatenate([t[:, :, 0, :128], t[:, :, 1, :128], t[:, :, 0, 128:], t[:, :, 1, 128:]], axis=-1)
-    out, marg = solve(own, bands, groups, nband)
-    vec = out[..., : 2 * ng].reshape(groups, planes, ng, 2, ng).transpose(0, 3, 1, 2, 4)
-    vectors = vec.reshape(bands, local)
+    out, marg = solve(orbitals.reshape(bands, local // 128, 128), ng, groups, nband)
+    vectors = out.reshape(bands, local)
     margin = marg[:, :bands].reshape(nband // groups, groups, bands).transpose(0, 2, 1).reshape(nband, groups)
     return (vectors, margin)
 

time: 68.6 us -> 60.6 us (0.88)
  Pallas kernels: 59.1 us -> 54.6 us
  local copies, waits for them, and re-layouts: 7.63 us -> 5.04 us
  other arithmetic: 0.87 us -> 0 us
    reshape x5 -> x0, local copies, waits for them, and re-layouts: 6.15 us -> none  [the longest x3 2.84 us: on_device(): orbitals.reshape(bands, 2, planes, ng, ng).transpose(2, 3, 1, 0, 4)]
    pallas_call x1, Pallas kernels: 59.1 us -> 54.6 us  [solve(): pl.pallas_call(functools.partial(solve_kernel, ng, ng ** 3), out_shape=(j...]
    unnamed x0 -> x4, local copies, waits for them, and re-layouts: none -> 4.37 us
    concatenate x1 -> x0, other arithmetic: 0.87 us -> none  [on_device(): jnp.concatenate([t[:, :, 0, :128], t[:, :, 1, :128], t[:, :, 0, 128:], t[...]
where the time goes in v3:
time: 60.6 us; the launch traced here: 60.3 us
  Pallas kernels  54.6 us (90%)
  local copies, waits for them, and re-layouts  5.04 us (8%)
  between operations  0.64 us (1%)
    pallas_call x1, Pallas kernels, solve(): pl.pallas_call(functools.partial(solve_kernel, ng, ng ** 3), out_shape=(j...  54.6 us
    unnamed x4, local copies, waits for them, and re-layouts  4.37 us

profile of v3, /device:TPU:0, one launch (start us, length us, event | category | flops | bytes accessed | tf_op | source)
XLA Modules:
  0.0 60.3 jit_solution(3798139028162798327)
XLA Ops:
  0.6 1.8 %copy.20 = f32[1,4,216,128]{3,2,1,0:T(8,128)} copy(f32[1,4,216,128]{3,1,2,0:T(4,128)} %bitcast.16) | data formatting | bytes 884736
  2.4 54.6 %solve.1 = (f32[4,216,128]{2,1,0:T(8,128)}, f32[8,128]{1,0:T(8,128)}) custom-call(f32[4,216,128]{2,1,0:T(8,128)} %bitcast.18, f32[25,48,128]{2,1,0:T(8,128)} %constant.14.clone.refs_0_, f32[25,24,128]{2,1,0:T(8,128)} %constant.15.clone.refs_1_, bf16[2,2,256,256]{3,2,1,0:T(8,128)(2,1)} %constant.16.clone.refs_2_, bf16[48,144]{1,0:T(8,128)(2,1)} %constant.17.clone.refs_3_, ...), custom_call_target="tpu_custom_call" | custom-call | flops 99999997952 | bytes 10000000 | tf_op jit(solution)/shard_map/solve/pallas_call | solution.py:662
  57.1 1.9 %copy.19 = f32[1,4,216,128]{3,1,2,0:T(4,128)} copy(f32[1,4,216,128]{3,2,1,0:T(8,128)} %bitcast.17) | data formatting | bytes 884736
  58.9 0.0 copy-start
  59.0 0.7 %copy-done = f32[8,128]{1,0:T(8,128)S(1)} copy-done((f32[8,128]{1,0:T(8,128)S(1)}, f32[8,128]{1,0:T(8,128)}, u32[]{:S(2)}) %copy-start) | copy-done | bytes 4120
  59.6 0.7 %reshape.19 = f32[8,4]{0,1:T(4,128)} reshape(f32[2,4,4]{1,0,2:T(2,128)S(1)} %bitcast.20) | data formatting | bytes 256 | tf_op jit(solution)/shard_map/reshape | solution.py:696
  (1 shorter events, 0.0 us)
Async XLA Ops:
  58.9 0.7 %copy-start = (f32[8,128]{1,0:T(8,128)S(1)}, f32[8,128]{1,0:T(8,128)}, u32[]{:S(2)}) copy-start(f32[8,128]{1,0:T(8,128)} %get-tuple-element.5) | copy-start | bytes 12292

commit v4 on v3

--- a/solution.py
+++ b/solution.py
@@ -114,15 +114,18 @@
     return jnp.dot(a, b, preferred_element_type=jnp.float32)
 
 
-def solve_kernel(ng, ncell, nat_ref, *refs):
+def solve_kernel(ng, ncell, in_ref, *refs):
     tables, refs = refs[:7], refs[7:]
-    (o_ref, m_ref, k1_ref, k2_ref, zt_ref, ty_ref, cp_ref, s_ref, hot_ref, own_ref, store, amp, acc, work, vec, recv, sel,
-     rows_buf, mine, marg, rsem, ssem, gsem, ysem, usem, dsem, wsem, osem, orsem, msem, mrsem, lsem, csem, esem, tmp, ebuf) = refs
+    (o_ref, m_ref, nat_ref, k1_ref, k2_ref, zt_ref, ty_ref, cp_ref, s_ref, hot_ref, own_ref, store, amp, acc, work, vec, recv, sel,
+     rows_buf, mine, marg, rsem, ssem, gsem, ysem, usem, dsem, wsem, osem, orsem, msem, mrsem, lsem, csem, esem, isem, tmp, ebuf) = refs
+    inputs = [pltpu.make_async_copy(in_ref.at[:, b], nat_ref.at[b], isem.at[b]) for b in range(in_ref.shape[1])]
+    for copy in inputs:
+        copy.start()
     kept = (k1_ref, k2_ref, zt_ref, ty_ref, cp_ref, s_ref, hot_ref)
     loads = [pltpu.make_async_copy(src, dst, csem.at[n]) for n, (src, dst) in enumerate(zip(tables, kept))]
     for n in (4, 2, 3, 0, 1, 5, 6):
         loads[n].start()
-    bands = nat_ref.shape[0]
+    bands = in_ref.shape[1]
     flat, width = own_ref.shape
     planes = flat // ng
     groups = vec.shape[0]
@@ -266,6 +269,8 @@
     def put_own(j, y0, value):
         ebuf[0, j, spaced(y0), :] = value
 
+    for copy in inputs:
+        copy.wait()
     gather_in(lambda b, h, q: nat_ref[b, packed(h, q), :], put_own, jnp.zeros((group, 128), jnp.float32))
     own_ref[...] = jnp.concatenate([ebuf[0, j] for j in range(3)], axis=1)
     pl.semaphore_wait(barrier, count)
@@ -510,13 +515,14 @@
     lax.fori_loop(3, length, later, 0)
 
     def emit(src, slot):
-        return pltpu.make_async_copy(src.at[slot], o_ref.at[slot], esem.at[slot])
+        return pltpu.make_async_copy(src.at[slot], o_ref.at[:, slot], esem.at[slot])
 
     def spread_out(src, slot, n):
         def put(j, y0, value):
             ebuf[n, j, spaced(y0), :] = value
 
-        gather_in(lambda b, h, q: src[slot, packed(h, q), :], put, jnp.zeros((group, 128), jnp.float32))
+        values = {(h, q): src[slot, packed(h, q), :] for h in range(2) for q in range(3)}
+        gather_in(lambda b, h, q: values[h, q], put, jnp.zeros((group, 128), jnp.float32))
 
     def columns(block, slots):
         parts = [[jnp.zeros((8, 128), jnp.float32) for _ in range(3)] for _ in slots]
@@ -526,7 +532,7 @@
                 for n, p in enumerate(parts):
                     p[j] = p[j] + phi * ebuf[n, j, pl.ds(8 * r, 8)]
         for slot, p in zip(slots, parts):
-            rows_buf[block, slot] = jnp.concatenate(p, axis=1)
+            rows_buf[slot, block] = jnp.concatenate(p, axis=1)
 
     def ready(block):
         near_by = jnp.logical_or(block == pair, block == third)
@@ -575,7 +581,14 @@
         hi = left_over.astype(jnp.bfloat16)
         terms += mm(hi, hot_ref[...])
         left_over = left_over - hi.astype(jnp.float32)
-    mine[...] = (terms / ncell).reshape(groups, nband, terms.shape[-1])
+    terms = (terms / ncell).reshape(groups, nband, terms.shape[-1])
+    each = nband // groups
+    for slot in range(groups):
+        total = jnp.zeros((groups, terms.shape[-1]), jnp.float32)
+        for n in range(each):
+            value = terms[:, slot * each + n]
+            total += pltpu.roll(value, bands * n, 1) if n else value
+        mine[slot] = total
 
     def give(slot):
         return remote(mine.at[slot], marg.at[me], msem.at[slot], mrsem.at[me], (band, slot))
@@ -610,7 +623,7 @@
     for slot in (sib, cross, far):
         remote(mine.at[slot], marg.at[slot], msem.at[slot], mrsem.at[slot], (band, slot)).wait()
         total += marg[slot]
-    m_ref[...] = total
+    m_ref[...] = total[:, :nband]
 
 
 def lane_tables(ng, bands):
@@ -634,9 +647,9 @@
 
 
 def solve(nat, ng, groups, nband):
-    bands = nat.shape[0]
+    bands = nat.shape[1]
     width = 2 * bands * ng
-    flat = nat.shape[1] * nat.shape[2] // (2 * ng)
+    flat = nat.shape[0] * nat.shape[2] // (2 * ng)
     half, bnd, zed = lane_tables(ng, bands)
     ht = hartley(ng)
     th, tl = split_const(ht)
@@ -657,25 +670,25 @@
     b16 = jnp.bfloat16
     consts = [k1, k2, zt, ty, cp.astype(b16), s.astype(b16), hot.astype(b16)]
     full = (groups, flat, width)
-    slim = (groups,) + nat.shape[1:]
+    slim = (groups, nat.shape[0], nat.shape[2])
     f32, dma = jnp.float32, pltpu.SemaphoreType.DMA
     return pl.pallas_call(
         functools.partial(solve_kernel, ng, ng**3),
         out_shape=(
-            jax.ShapeDtypeStruct(slim, f32), jax.ShapeDtypeStruct((nband, 128), f32)
+            jax.ShapeDtypeStruct(nat.shape, f32), jax.ShapeDtypeStruct((groups, nband), f32)
         ),
-        in_specs=[pl.BlockSpec(memory_space=pltpu.VMEM)] + [pl.BlockSpec(memory_space=pl.ANY)] * len(consts),
+        in_specs=[pl.BlockSpec(memory_space=pl.ANY)] * (1 + len(consts)),
         out_specs=(pl.BlockSpec(memory_space=pl.ANY), pl.BlockSpec(memory_space=pltpu.VMEM)),
         scratch_shapes=[
-            *[pltpu.VMEM(c.shape, c.dtype) for c in consts],
+            pltpu.VMEM((bands,) + slim[1:], f32), *[pltpu.VMEM(c.shape, c.dtype) for c in consts],
             pltpu.VMEM(full[1:], f32), pltpu.VMEM((nband + 3 * groups,) + full[1:], f32),
             pltpu.VMEM(full, f32), pltpu.VMEM(full, f32), pltpu.VMEM((groups, flat // ng, ng, width), f32),
             pltpu.VMEM(slim, f32), pltpu.VMEM(slim, f32),
-            pltpu.VMEM((2, 256, 256), b16), pltpu.VMEM((nband, groups, 8, width), f32),
-            pltpu.VMEM((groups, nband, 128), f32), pltpu.VMEM((groups, nband, 128), f32),
+            pltpu.VMEM((2, 256, 256), b16), pltpu.VMEM((groups, nband, 8, width), f32),
+            pltpu.VMEM((groups, groups, 128), f32), pltpu.VMEM((groups, groups, 128), f32),
             dma((3, groups, 2)), dma((3, 3, 2)), dma((nband, 2)), dma((nband, 2)), dma((nband, 2)), dma((nband, 2)),
             dma((nband, 2)),
-            dma((groups,)), dma((groups,)), dma((groups,)), dma((groups,)), dma(()), dma((len(consts),)), dma((groups,)),
+            dma((groups,)), dma((groups,)), dma((groups,)), dma((groups,)), dma(()), dma((len(consts),)), dma((groups,)), dma((bands,)),
             pltpu.VMEM((flat, 128), f32), pltpu.VMEM((2, 3, flat, 128), f32),
         ],
         compiler_params=pltpu.CompilerParams(
@@ -691,9 +704,10 @@
     bands, local = orbitals.shape
     ncell = local * groups
     ng = round(ncell ** (1 / 3))
-    out, marg = solve(orbitals.reshape(bands, local // 128, 128), ng, groups, nband)
-    vectors = out.reshape(bands, local)
-    margin = marg[:, :bands].reshape(nband // groups, groups, bands).transpose(0, 2, 1).reshape(nband, groups)
+    nat = orbitals.reshape(bands, local // 128, 128).transpose(1, 0, 2)
+    out, marg = solve(nat, ng, groups, nband)
+    vectors = out.transpose(1, 0, 2).reshape(bands, local)
+    margin = marg.T
     return (vectors, margin)
 
 

time: 60.6 us -> 56.9 us (0.939)
  local copies, waits for them, and re-layouts: 5.04 us -> 2.39 us
  Pallas kernels: 54.6 us -> 53.7 us
    unnamed x4, local copies, waits for them, and re-layouts: 4.37 us -> 2.39 us
    pallas_call x1, Pallas kernels: 54.6 us -> 53.7 us  [solve(): pl.pallas_call(functools.partial(solve_kernel, ng, ng ** 3), out_shape=(j...]
    reshape x1 -> x0, local copies, waits for them, and re-layouts: 0.66 us -> none  [on_device(): marg[:, :bands].reshape(nband // groups, groups, bands).transpose(0, 2, 1)]
where the time goes in v4:
time: 56.9 us; the launch traced here: 56.7 us
  Pallas kernels  53.7 us (94%)
  local copies, waits for them, and re-layouts  2.39 us (4%)
  between operations  0.65 us (1%)
    pallas_call x1, Pallas kernels, solve(): pl.pallas_call(functools.partial(solve_kernel, ng, ng ** 3), out_shape=(j...  53.7 us
    unnamed x4, local copies, waits for them, and re-layouts  2.39 us

profile of v4, /device:TPU:0, one launch (start us, length us, event | category | flops | bytes accessed | tf_op | source)
XLA Modules:
  0.0 56.7 jit_solution(430015155666268513)
XLA Ops:
  0.6 53.7 %solve.1 = (f32[216,4,128]{2,1,0:T(4,128)}, f32[4,8]{1,0:T(4,128)}) custom-call(f32[216,4,128]{2,1,0:T(4,128)} %bitcast.9, f32[25,48,128]{2,1,0:T(8,128)} %constant.14.clone.refs_0_, f32[25,24,128]{2,1,0:T(8,128)} %constant.15.clone.refs_1_, bf16[2,2,256,256]{3,2,1,0:T(8,128)(2,1)} %constant.16.clone.refs_2_, bf16[48,144]{1,0:T(8,128)(2,1)} %constant.17.clone.refs_3_, ...), custom_call_target="tpu_custom_call" | custom-call | flops 99999997952 | bytes 10000000 | tf_op jit(solution)/shard_map/solve/pallas_call | solution.py:675
  54.3 0.0 copy-start
  54.4 1.8 %copy.12 = f32[4,27648]{1,0:T(4,128)} copy(f32[4,27648]{1,0:T(4,128)} %bitcast.7) | data formatting | bytes 884736
  56.2 0.0 copy-done
  56.2 0.6 %copy.13 = f32[8,4]{0,1:T(4,128)} copy(f32[8,4]{0,1:T(4,128)S(1)} %bitcast.8) | data formatting | bytes 256
Async XLA Ops:
  54.3 1.8 %copy-start = (f32[4,8]{1,0:T(4,128)S(1)}, f32[4,8]{1,0:T(4,128)}, u32[]{:S(2)}) copy-start(f32[4,8]{1,0:T(4,128)} %get-tuple-element.5) | copy-start | bytes 388

commit v5 on v4

--- a/solution.py
+++ b/solution.py
@@ -114,17 +114,24 @@
     return jnp.dot(a, b, preferred_element_type=jnp.float32)
 
 
+def in_copies(in_ref, nat_ref, sems, c):
+    size = nat_ref.shape[3]
+    return [
+        pltpu.make_async_copy(in_ref.at[pl.ds((2 * h + c) * size, size), b], nat_ref.at[h, c, b], sems.at[h, c, b])
+        for h in range(2)
+        for b in range(in_ref.shape[1])
+    ]
+
+
 def solve_kernel(ng, ncell, in_ref, *refs):
-    tables, refs = refs[:7], refs[7:]
-    (o_ref, m_ref, nat_ref, k1_ref, k2_ref, zt_ref, ty_ref, cp_ref, s_ref, hot_ref, own_ref, store, amp, acc, work, vec, recv, sel,
-     rows_buf, mine, marg, rsem, ssem, gsem, ysem, usem, dsem, wsem, osem, orsem, msem, mrsem, lsem, csem, esem, isem, tmp, ebuf) = refs
-    inputs = [pltpu.make_async_copy(in_ref.at[:, b], nat_ref.at[b], isem.at[b]) for b in range(in_ref.shape[1])]
-    for copy in inputs:
+    (k_hbm, t_hbm, o_ref, m_ref, nat_ref, k_ref, t_ref, own_ref, store, amp, acc, work, vec, recv, sel, rows_buf, mine, marg,
+     rsem, ssem, gsem, ysem, usem, dsem, wsem, osem, orsem, msem, mrsem, lsem, csem, esem, isem, tmp, ebuf) = refs
+    for copy in in_copies(in_ref, nat_ref, isem, 0) + in_copies(in_ref, nat_ref, isem, 1):
         copy.start()
-    kept = (k1_ref, k2_ref, zt_ref, ty_ref, cp_ref, s_ref, hot_ref)
-    loads = [pltpu.make_async_copy(src, dst, csem.at[n]) for n, (src, dst) in enumerate(zip(tables, kept))]
-    for n in (4, 2, 3, 0, 1, 5, 6):
-        loads[n].start()
+    load_t = pltpu.make_async_copy(t_hbm, t_ref, csem.at[0])
+    load_k = pltpu.make_async_copy(k_hbm, k_ref, csem.at[1])
+    load_t.start()
+    load_k.start()
     bands = in_ref.shape[1]
     flat, width = own_ref.shape
     planes = flat // ng
@@ -146,6 +153,9 @@
     up, down = jnp.where(has_up, band + 2, band), jnp.where(has_down, band - 2, band)
     mesh_id = pl.DeviceIdType.MESH
     part = planes // 2
+    zrow, crow = 256, 1024
+    srow = crow + 512
+    yrow = srow + width
 
     def remote(src, dst, send, recv_sem, device):
         return pltpu.make_async_remote_copy(
@@ -266,15 +276,21 @@
                 copy = along(band, wsem, wrap, c, own_ref)
                 copy.start() if act == "go" else copy.wait_send()
 
-    def put_own(j, y0, value):
-        ebuf[0, j, spaced(y0), :] = value
-
-    for copy in inputs:
-        copy.wait()
-    gather_in(lambda b, h, q: nat_ref[b, packed(h, q), :], put_own, jnp.zeros((group, 128), jnp.float32))
-    own_ref[...] = jnp.concatenate([ebuf[0, j] for j in range(3)], axis=1)
-    pl.semaphore_wait(barrier, count)
+    few = group // 2
     for c in range(2):
+        for copy in in_copies(in_ref, nat_ref, isem, c):
+            copy.wait()
+
+        def put_own(j, y0, value):
+            ebuf[0, j, pl.ds(c * part * ng + y0, few, stride=8), :] = value
+
+        gather_in(
+            lambda b, h, q: nat_ref[h, c, b, pl.ds(q, few, stride=3), :], put_own, jnp.zeros((few, 128), jnp.float32)
+        )
+        half_rows = pl.ds(c * part * ng, part * ng)
+        own_ref[half_rows, :] = jnp.concatenate([ebuf[0, j, half_rows, :] for j in range(3)], axis=1)
+        if c == 0:
+            pl.semaphore_wait(barrier, count)
         own_copies(c, "go")
     wrap_copies("go")
     local = pltpu.make_async_copy(own_ref, store.at[band], lsem)
@@ -333,12 +349,13 @@
         parts = []
         for h in range(2):
             a, b = (jnp.concatenate([t[:, 128 * h:128 * h + 128], t[:, 256:]], axis=1) for t in (hi, lo))
-            parts.append(mm(a, zt_ref[h, 0]) + mm(b, zt_ref[h, 0]) + mm(a, zt_ref[h, 1]))
+            high, low = (t_ref[pl.ds((2 * h + n) * zrow, zrow), :] for n in range(2))
+            parts.append(mm(a, high) + mm(b, high) + mm(a, low))
         return jnp.concatenate([parts[0][:, :128], parts[1][:, :128], parts[0][:, 128:] + parts[1][:, 128:]], axis=1)
 
     def ytrans(v):
         hi, lo = split(v)
-        return mm(ty_ref[...], jnp.concatenate([hi, lo, hi], axis=0))
+        return mm(t_ref[pl.ds(yrow, ng), pl.ds(0, 3 * ng)], jnp.concatenate([hi, lo, hi], axis=0))
 
     def amplitude(v):
         hi, lo = split(v)
@@ -348,11 +365,10 @@
             parts.append(mm(a, sel[h]) + mm(b, sel[h]))
         return jnp.concatenate([parts[0][:, :128], parts[1][:, :128], parts[0][:, 128:] + parts[1][:, 128:]], axis=1)
 
-    for n in (4, 2, 3):
-        loads[n].wait()
+    load_t.wait()
     for h in range(2):
         mark = (me + 1).astype(jnp.float32)
-        sel[h] = jnp.where(cp_ref[h].astype(jnp.float32) == mark, 1.0, 0.0).astype(jnp.bfloat16)
+        sel[h] = jnp.where(t_ref[pl.ds(crow + zrow * h, zrow), :].astype(jnp.float32) == mark, 1.0, 0.0).astype(jnp.bfloat16)
 
     def transform(blk, slots, c):
         rows = pl.ds(c * part * ng, part * ng)
@@ -415,7 +431,7 @@
         for i in range(2):
             rows = pl.ds(pl.multiple_of(t * 16 + 8 * i, 8), 8)
             res = conv([work[g, r, rows, h * 128:h * 128 + 128] for g, h, r in order],
-                       lambda k: k1_ref[k, rows, :])
+                       lambda k: k_ref[k, rows, :])
             for (g, h, r), v in zip(order, res):
                 work[g, r, rows, h * 128:h * 128 + 128] = v
         ra = pl.ds(pl.multiple_of(t * 16, 8), 8)
@@ -428,8 +444,8 @@
                 return jnp.where(left, u, pltpu.roll(w, 64, 1))
             return jnp.where(left, pltpu.roll(u, 64, 1), w)
 
-        rk = pl.ds(pl.multiple_of(t * 8, 8), 8)
-        res = dict(zip(order, conv([half(*o) for o in order], lambda k: k2_ref[k, rk, :])))
+        rk = pl.ds(pl.multiple_of(ng + t * 8, 8), 8)
+        res = dict(zip(order, conv([half(*o) for o in order], lambda k: k_ref[k, rk, :])))
         for g in range(4):
             for r in range(planes):
                 a, b = res[(g, 0, r)], res[(g, 1, r)]
@@ -460,7 +476,8 @@
         @pl.when(blk == 2)
         def _():
             hi, lo = split(acc[slot] + w)
-            tmp[...] = -(mm(hi, s_ref[...]) + mm(lo, s_ref[...]))
+            s_tab = t_ref[pl.ds(srow, width), pl.ds(0, 128)]
+            tmp[...] = -(mm(hi, s_tab) + mm(lo, s_tab))
 
             def put_vec(h, q, value):
                 vec[slot, packed(h, q), :] = value
@@ -497,8 +514,7 @@
 
         @pl.when(blk == 0)
         def _():
-            for n in (0, 1, 5, 6):
-                loads[n].wait()
+            load_k.wait()
 
         lax.fori_loop(0, ng // 16, mid, 0)
         lax.fori_loop(0, 4, inv, 0)
@@ -576,10 +592,10 @@
 
     lanes = jnp.sum(rows_buf[...], axis=2).reshape(groups * nband, width)
     left_over = lanes
-    terms = jnp.zeros((groups * nband, hot_ref.shape[-1]), jnp.float32)
+    terms = jnp.zeros((groups * nband, 128), jnp.float32)
     for _ in range(3):
         hi = left_over.astype(jnp.bfloat16)
-        terms += mm(hi, hot_ref[...])
+        terms += mm(hi, t_ref[pl.ds(srow, width), pl.ds(128, 128)])
         left_over = left_over - hi.astype(jnp.float32)
     terms = (terms / ncell).reshape(groups, nband, terms.shape[-1])
     each = nband // groups
@@ -668,7 +684,10 @@
     rest = kb[:, :, 128:].reshape(kb.shape[0], ng // 16, 2, 8, 64)
     k2 = np.concatenate([rest[:, :, 0], rest[:, :, 1]], axis=-1).reshape(kb.shape[0], ng // 2, 128)
     b16 = jnp.bfloat16
-    consts = [k1, k2, zt, ty, cp.astype(b16), s.astype(b16), hot.astype(b16)]
+    tyw = np.zeros((ng, 256), b16)
+    tyw[:, : 3 * ng] = ty
+    tab = [zt.reshape(-1, 256), cp.astype(b16).reshape(-1, 256), np.concatenate([s, hot], axis=1).astype(b16), tyw]
+    consts = [np.concatenate([k1, k2], axis=1), np.concatenate(tab, axis=0)]
     full = (groups, flat, width)
     slim = (groups, nat.shape[0], nat.shape[2])
     f32, dma = jnp.float32, pltpu.SemaphoreType.DMA
@@ -680,7 +699,7 @@
         in_specs=[pl.BlockSpec(memory_space=pl.ANY)] * (1 + len(consts)),
         out_specs=(pl.BlockSpec(memory_space=pl.ANY), pl.BlockSpec(memory_space=pltpu.VMEM)),
         scratch_shapes=[
-            pltpu.VMEM((bands,) + slim[1:], f32), *[pltpu.VMEM(c.shape, c.dtype) for c in consts],
+            pltpu.VMEM((2, 2, bands, slim[1] // 4, 128), f32), *[pltpu.VMEM(c.shape, c.dtype) for c in consts],
             pltpu.VMEM(full[1:], f32), pltpu.VMEM((nband + 3 * groups,) + full[1:], f32),
             pltpu.VMEM(full, f32), pltpu.VMEM(full, f32), pltpu.VMEM((groups, flat // ng, ng, width), f32),
             pltpu.VMEM(slim, f32), pltpu.VMEM(slim, f32),
@@ -688,11 +707,11 @@
             pltpu.VMEM((groups, groups, 128), f32), pltpu.VMEM((groups, groups, 128), f32),
             dma((3, groups, 2)), dma((3, 3, 2)), dma((nband, 2)), dma((nband, 2)), dma((nband, 2)), dma((nband, 2)),
             dma((nband, 2)),
-            dma((groups,)), dma((groups,)), dma((groups,)), dma((groups,)), dma(()), dma((len(consts),)), dma((groups,)), dma((bands,)),
+            dma((groups,)), dma((groups,)), dma((groups,)), dma((groups,)), dma(()), dma((len(consts),)), dma((groups,)), dma((2, 2, bands)),
             pltpu.VMEM((flat, 128), f32), pltpu.VMEM((2, 3, flat, 128), f32),
         ],
         compiler_params=pltpu.CompilerParams(
-            vmem_limit_bytes=60 * 1024 * 1024, collective_id=0, has_side_effects=True
+            vmem_limit_bytes=55_800_000, collective_id=0, has_side_effects=True
         ),
         cost_estimate=pl.CostEstimate(flops=10**11, bytes_accessed=10**7, transcendentals=0),
         name="solve",

time: 56.9 us -> 55.2 us (0.970)
  local copies, waits for them, and re-layouts: 2.39 us -> 1.34 us
  Pallas kernels: 53.7 us -> 53.1 us
    unnamed x4 -> x2, local copies, waits for them, and re-layouts: 2.39 us -> 1.34 us
    pallas_call x1, Pallas kernels: 53.7 us -> 53.1 us  [solve(): pl.pallas_call(functools.partial(solve_kernel, ng, ng ** 3), out_shape=(j...]
where the time goes in v5:
time: 55.2 us; the launch traced here: 55.1 us
  Pallas kernels  53.1 us (96%)
  local copies, waits for them, and re-layouts  1.34 us (2%)
  between operations  0.64 us (1%)
    pallas_call x1, Pallas kernels, solve(): pl.pallas_call(functools.partial(solve_kernel, ng, ng ** 3), out_shape=(j...  53.1 us
    unnamed x2, local copies, waits for them, and re-layouts  1.34 us

profile of v5, /device:TPU:0, one launch (start us, length us, event | category | flops | bytes accessed | tf_op | source)
XLA Modules:
  0.0 55.1 jit_solution(8041280005407423938)
XLA Ops:
  0.6 53.1 %solve.1 = (f32[216,4,128]{2,1,0:T(4,128)S(1)}, f32[4,8]{1,0:T(4,128)S(1)}) custom-call(f32[216,4,128]{2,1,0:T(4,128)} %bitcast.9, f32[25,72,128]{2,1,0:T(8,128)} %constant.4.clone.refs_0_, bf16[1968,256]{1,0:T(8,128)(2,1)} %constant.5.clone.refs_1_), custom_call_target="tpu_custom_call" | custom-call | flops 99999997952 | bytes 10000000 | tf_op jit(solution)/shard_map/solve/pallas_call | solution.py:694
  53.7 0.8 %copy.7 = f32[4,27648]{1,0:T(4,128)} copy(f32[4,27648]{1,0:T(4,128)S(1)} %bitcast.7) | data formatting | bytes 884736
  54.5 0.6 %copy.8 = f32[8,4]{0,1:T(4,128)} copy(f32[8,4]{0,1:T(4,128)S(1)} %bitcast.8) | data formatting | bytes 256

commit v6 on v5

--- a/solution.py
+++ b/solution.py
@@ -117,7 +117,7 @@
 def in_copies(in_ref, nat_ref, sems, c):
     size = nat_ref.shape[3]
     return [
-        pltpu.make_async_copy(in_ref.at[pl.ds((2 * h + c) * size, size), b], nat_ref.at[h, c, b], sems.at[h, c, b])
+        pltpu.make_async_copy(in_ref.at[pl.ds((2 * h + c) * size, size), b], nat_ref.at[c, h, b], sems.at[c])
         for h in range(2)
         for b in range(in_ref.shape[1])
     ]
@@ -125,7 +125,7 @@
 
 def solve_kernel(ng, ncell, in_ref, *refs):
     (k_hbm, t_hbm, o_ref, m_ref, nat_ref, k_ref, t_ref, own_ref, store, amp, acc, work, vec, recv, sel, rows_buf, mine, marg,
-     rsem, ssem, gsem, ysem, usem, dsem, wsem, osem, orsem, msem, mrsem, lsem, csem, esem, isem, tmp, ebuf) = refs
+     rsem, ssem, gsem, ysem, zsem, dsem, wsem, osem, orsem, msem, mrsem, lsem, csem, esem, isem, tmp, ebuf) = refs
     for copy in in_copies(in_ref, nat_ref, isem, 0) + in_copies(in_ref, nat_ref, isem, 1):
         copy.start()
     load_t = pltpu.make_async_copy(t_hbm, t_ref, csem.at[0])
@@ -172,17 +172,20 @@
     def piece(ref, c):
         return ref.at[pl.ds(c * part * ng, part * ng)]
 
+    def skip(slot, at):
+        return slot - (slot > at).astype(jnp.int32)
+
     def share(blk, lane, slot, src, target, c):
         dst = store.at[nband + blk * groups + slot]
-        return remote(piece(src, c), piece(dst, c), ssem.at[blk, lane, c], rsem.at[blk, slot, c], (band, target))
-
-    def along(block, sems, device, c, src=None):
+        return remote(piece(src, c), piece(dst, c), ssem.at[lane], rsem.at[blk, skip(slot, target), c], (band, target))
+
+    def along(block, sem, device, c, src=None):
         dst = store.at[block]
         src = dst if src is None else src
-        return remote(piece(src, c), piece(dst, c), sems.at[block, c], gsem.at[block, c], (device, me))
+        return remote(piece(src, c), piece(dst, c), sem, gsem.at[block, c], (device, me))
 
     def came(block, c):
-        along(block, ysem, pair, c).wait_recv()
+        along(block, wsem, pair, c).wait_recv()
 
     lane = lax.broadcasted_iota(jnp.int32, (1, 128), 1)
 
@@ -253,51 +256,46 @@
         greet((wrap, me))
 
     count = 4 + has_up.astype(jnp.int32) + has_down.astype(jnp.int32) + ends.astype(jnp.int32)
-    def own_copies(c, act):
-        def go(copy):
-            copy.start() if act == "go" else copy.wait_send()
-
-        go(share(0, 1, me, own_ref, cross, c))
-        go(share(0, 0, me, own_ref, sib, c))
-        go(along(band, ysem, pair, c, own_ref))
+    def own_copies(c):
+        share(0, 1, me, own_ref, cross, c).start()
+        share(0, 0, me, own_ref, sib, c).start()
+        along(band, ysem.at[pos, c], pair, c, own_ref).start()
 
         @pl.when(has_up)
         def _():
-            go(along(band, usem, up, c, own_ref))
+            along(band, zsem.at[pos, c], up, c, own_ref).start()
 
         @pl.when(has_down)
         def _():
-            go(along(band, dsem, down, c, own_ref))
-
-    def wrap_copies(act):
-        @pl.when(ends)
-        def _():
-            for c in range(2):
-                copy = along(band, wsem, wrap, c, own_ref)
-                copy.start() if act == "go" else copy.wait_send()
+            along(band, dsem, down, c, own_ref).start()
 
     few = group // 2
     for c in range(2):
-        for copy in in_copies(in_ref, nat_ref, isem, c):
-            copy.wait()
+        pltpu.make_async_copy(nat_ref.at[c], nat_ref.at[c], isem.at[c]).wait()
 
         def put_own(j, y0, value):
             ebuf[0, j, pl.ds(c * part * ng + y0, few, stride=8), :] = value
 
         gather_in(
-            lambda b, h, q: nat_ref[h, c, b, pl.ds(q, few, stride=3), :], put_own, jnp.zeros((few, 128), jnp.float32)
+            lambda b, h, q: nat_ref[c, h, b, pl.ds(q, few, stride=3), :], put_own, jnp.zeros((few, 128), jnp.float32)
         )
         half_rows = pl.ds(c * part * ng, part * ng)
         own_ref[half_rows, :] = jnp.concatenate([ebuf[0, j, half_rows, :] for j in range(3)], axis=1)
         if c == 0:
             pl.semaphore_wait(barrier, count)
-        own_copies(c, "go")
-    wrap_copies("go")
+        own_copies(c)
+
+    @pl.when(ends)
+    def _():
+        for c in range(2):
+            along(band, wsem, wrap, c, own_ref).start()
+
     local = pltpu.make_async_copy(own_ref, store.at[band], lsem)
     local.start()
 
     def arrived(blk, slot, c):
-        share(blk, 0, slot, own_ref, sib, c).wait_recv()
+        dst = piece(store.at[nband + blk * groups + slot], c)
+        remote(dst, dst, ssem.at[0], rsem.at[blk, skip(slot, me), c], (band, sib)).wait_recv()
 
     def relay(blk, c):
         arrived(blk, cross, c)
@@ -314,7 +312,7 @@
         )
 
     def line(d, c, near, act):
-        def pass_on(block, exists, on, sems, device):
+        def pass_on(block, exists, on, device):
             @pl.when(exists)
             def _():
                 if act == "go":
@@ -325,16 +323,16 @@
 
                 @pl.when(jnp.logical_not(skipped(block)))
                 def _():
-                    one(along(block, ysem, pair, c))
+                    one(along(block, ysem.at[block // 2, c], pair, c))
 
                 @pl.when(on)
                 def _():
-                    one(along(block, sems, device, c))
+                    one(along(block, zsem.at[block // 2, c], device, c))
 
         upward = (side == 1) == near
-        pass_on(band - 2 * d, jnp.logical_and(upward, pos - d >= 0), has_up, usem, up)
+        pass_on(band - 2 * d, jnp.logical_and(upward, pos - d >= 0), has_up, up)
         pass_on(
-            band + 2 * d, jnp.logical_and(jnp.logical_not(upward), pos + d <= length - 1), has_down, dsem, down
+            band + 2 * d, jnp.logical_and(jnp.logical_not(upward), pos + d <= length - 1), has_down, down
         )
 
     def serve(blk, c):
@@ -453,7 +451,7 @@
                 work[g, r, rb, 256:384] = jnp.where(left, pltpu.roll(a, 64, 1), b)
 
     def push(slot):
-        return remote(vec.at[slot], recv.at[me], osem.at[slot], orsem.at[me], (band, slot))
+        return remote(vec.at[slot], recv.at[me], osem, orsem.at[me], (band, slot))
 
     def inverse(blk, s):
         slot = ((chip + 1 - s // 2) % 2) * 2 + (core + s % 2 + s // 2) % 2
@@ -531,7 +529,7 @@
     lax.fori_loop(3, length, later, 0)
 
     def emit(src, slot):
-        return pltpu.make_async_copy(src.at[slot], o_ref.at[:, slot], esem.at[slot])
+        return pltpu.make_async_copy(src.at[slot], o_ref.at[:, slot], esem)
 
     def spread_out(src, slot, n):
         def put(j, y0, value):
@@ -540,12 +538,15 @@
         values = {(h, q): src[slot, packed(h, q), :] for h in range(2) for q in range(3)}
         gather_in(lambda b, h, q: values[h, q], put, jnp.zeros((group, 128), jnp.float32))
 
+    order = (me, sib, cross, far)
+
     def columns(block, slots):
+        where = [next(n for n, s in enumerate(order) if s is slot) for slot in slots]
         parts = [[jnp.zeros((8, 128), jnp.float32) for _ in range(3)] for _ in slots]
         for r in range(flat // 8):
             for j in range(3):
                 phi = store[block, pl.ds(8 * r, 8), pl.ds(128 * j, 128)]
-                for n, p in enumerate(parts):
+                for n, p in zip(where, parts):
                     p[j] = p[j] + phi * ebuf[n, j, pl.ds(8 * r, 8)]
         for slot, p in zip(slots, parts):
             rows_buf[slot, block] = jnp.concatenate(p, axis=1)
@@ -554,42 +555,46 @@
         near_by = jnp.logical_or(block == pair, block == third)
         return jnp.logical_or(near_by, block % 2 == side)
 
-    def early(block, _):
-        @pl.when(ready(block))
-        def _():
-            columns(block, (me, sib))
-
-        return 0
+    def early(slots):
+        def body(block, _):
+            @pl.when(ready(block))
+            def _():
+                columns(block, slots)
+
+            return 0
+
+        return body
 
     def late(block, _):
         @pl.when(jnp.logical_not(ready(block)))
         def _():
             for c in range(2):
                 came(block, c)
-            columns(block, (me, sib))
+            columns(block, (me, sib, cross))
 
         return 0
 
-    def rest(block, _):
-        columns(block, (cross, far))
-        return 0
-
     def settle(slot):
-        remote(vec.at[slot], recv.at[slot], osem.at[slot], orsem.at[slot], (band, slot)).wait()
+        remote(vec.at[slot], recv.at[slot], osem, orsem.at[slot], (band, slot)).wait_recv()
         emit(recv, slot).start()
 
     emit(vec, me).start()
     spread_out(vec, me, 0)
     settle(sib)
     spread_out(recv, sib, 1)
-    lax.fori_loop(0, nband, early, 0)
+    lax.fori_loop(0, nband, early((me, sib)), 0)
+    settle(cross)
+    spread_out(recv, cross, 2)
+    lax.fori_loop(0, nband, early((cross,)), 0)
     lax.fori_loop(0, nband, late, 0)
-    settle(cross)
-    spread_out(recv, cross, 0)
     settle(far)
-    spread_out(recv, far, 1)
-    lax.fori_loop(0, nband, rest, 0)
-
+    spread_out(recv, far, 3)
+
+    def last(block, _):
+        columns(block, (far,))
+        return 0
+
+    lax.fori_loop(0, nband, last, 0)
     lanes = jnp.sum(rows_buf[...], axis=2).reshape(groups * nband, width)
     left_over = lanes
     terms = jnp.zeros((groups * nband, 128), jnp.float32)
@@ -607,37 +612,43 @@
         mine[slot] = total
 
     def give(slot):
-        return remote(mine.at[slot], marg.at[me], msem.at[slot], mrsem.at[me], (band, slot))
+        return remote(mine.at[slot], marg.at[me], msem, mrsem.at[me], (band, slot))
 
     for slot in (cross, far, sib):
         give(slot).start()
-    for slot in range(groups):
-        emit(recv, slot).wait()
-    wrap_copies("end")
+    pltpu.make_async_copy(o_ref, o_ref, esem).wait()
+    others = pl.ds(0, groups - 1)
+    remote(vec.at[others], recv.at[others], osem, orsem.at[me], (band, sib)).wait_send()
+    remote(mine.at[others], marg.at[others], msem, mrsem.at[me], (band, sib)).wait_send()
+    three = store.at[pl.ds(0, 3)]
+    for n in range(3):
+        remote(three, three, ssem.at[n], gsem.at[0, 0], (band, sib)).wait_send()
+    whole = store.at[band]
+
+    @pl.when(ends)
+    def _():
+        remote(whole, whole, wsem, gsem.at[0, 0], (wrap, me)).wait_send()
+
+    @pl.when(has_down)
+    def _():
+        remote(whole, whole, dsem, gsem.at[0, 0], (down, me)).wait_send()
+
     for c in range(2):
-        own_copies(c, "end")
-
-    def finish(i, _):
-        blk, c = 1 + i // 2, i % 2
-        for lane, target in ((0, sib), (1, cross)):
-            share(blk, lane, me, own_ref, target, c).wait_send()
-        return 0
-
-    def finish_relay(i, _):
-        share(i // 2, 2, me, own_ref, sib, i % 2).wait_send()
-        return 0
+        along(band, ysem.at[pos, c], pair, c).wait_send()
+
+        @pl.when(has_up)
+        def _():
+            along(band, zsem.at[pos, c], up, c).wait_send()
 
     def finish_line(i, _):
         line(1 + i // 2, i % 2, True, "end")
         line(1 + i // 2, i % 2, False, "end")
         return 0
 
-    lax.fori_loop(0, 4, finish, 0)
-    lax.fori_loop(0, 6, finish_relay, 0)
     lax.fori_loop(0, 2 * (length - 1), finish_line, 0)
     total = mine[me]
     for slot in (sib, cross, far):
-        remote(mine.at[slot], marg.at[slot], msem.at[slot], mrsem.at[slot], (band, slot)).wait()
+        remote(mine.at[slot], marg.at[slot], msem, mrsem.at[slot], (band, slot)).wait_recv()
         total += marg[slot]
     m_ref[...] = total[:, :nband]
 
@@ -705,10 +716,9 @@
             pltpu.VMEM(slim, f32), pltpu.VMEM(slim, f32),
             pltpu.VMEM((2, 256, 256), b16), pltpu.VMEM((groups, nband, 8, width), f32),
             pltpu.VMEM((groups, groups, 128), f32), pltpu.VMEM((groups, groups, 128), f32),
-            dma((3, groups, 2)), dma((3, 3, 2)), dma((nband, 2)), dma((nband, 2)), dma((nband, 2)), dma((nband, 2)),
-            dma((nband, 2)),
-            dma((groups,)), dma((groups,)), dma((groups,)), dma((groups,)), dma(()), dma((len(consts),)), dma((groups,)), dma((2, 2, bands)),
-            pltpu.VMEM((flat, 128), f32), pltpu.VMEM((2, 3, flat, 128), f32),
+            dma((3, groups - 1, 2)), dma((3,)), dma((nband, 2)), dma((nband // 2, 2)), dma((nband // 2, 2)), dma(()), dma(()),
+            dma(()), dma((groups,)), dma(()), dma((groups,)), dma(()), dma((2,)), dma(()), dma((2,)),
+            pltpu.VMEM((flat, 128), f32), pltpu.VMEM((groups, 3, flat, 128), f32),
         ],
         compiler_params=pltpu.CompilerParams(
             vmem_limit_bytes=55_800_000, collective_id=0, has_side_effects=True

time: 55.2 us -> 54.2 us (0.982)
  Pallas kernels: 53.1 us -> 52.1 us
    pallas_call x1, Pallas kernels: 53.1 us -> 52.1 us  [solve(): pl.pallas_call(functools.partial(solve_kernel, ng, ng ** 3), out_shape=(j...]
where the time goes in v6:
time: 54.2 us; the launch traced here: 54.1 us
  Pallas kernels  52.1 us (96%)
  local copies, waits for them, and re-layouts  1.34 us (2%)
  between operations  0.64 us (1%)
    pallas_call x1, Pallas kernels, solve(): pl.pallas_call(functools.partial(solve_kernel, ng, ng ** 3), out_shape=(j...  52.1 us
    unnamed x2, local copies, waits for them, and re-layouts  1.34 us

profile of v6, /device:TPU:0, one launch (start us, length us, event | category | flops | bytes accessed | tf_op | source)
XLA Modules:
  0.0 54.1 jit_solution(12457514085367248365)
XLA Ops:
  0.6 52.1 %solve.1 = (f32[216,4,128]{2,1,0:T(4,128)S(1)}, f32[4,8]{1,0:T(4,128)S(1)}) custom-call(f32[216,4,128]{2,1,0:T(4,128)} %bitcast.9, f32[25,72,128]{2,1,0:T(8,128)} %constant.4.clone.refs_0_, bf16[1968,256]{1,0:T(8,128)(2,1)} %constant.5.clone.refs_1_), custom_call_target="tpu_custom_call" | custom-call | flops 99999997952 | bytes 10000000 | tf_op jit(solution)/shard_map/solve/pallas_call | solution.py:705
  52.7 0.8 %copy.7 = f32[4,27648]{1,0:T(4,128)} copy(f32[4,27648]{1,0:T(4,128)S(1)} %bitcast.7) | data formatting | bytes 884736
  53.5 0.6 %copy.8 = f32[8,4]{0,1:T(4,128)} copy(f32[8,4]{0,1:T(4,128)S(1)} %bitcast.8) | data formatting | bytes 256

commit v7 on v6

--- a/solution.py
+++ b/solution.py
@@ -31,10 +31,8 @@
 
 def rfft(xs):
     n = len(xs)
-    if n == 3:
-        s = xs[1] + xs[2]
-        d = xs[1] - xs[2]
-        return [(xs[0] + s, None), (xs[0] - 0.5 * s, d * (-np.sqrt(3.0) / 2))]
+    if n == 1:
+        return [(xs[0], None)]
     even, odd = rfft(xs[0::2]), rfft(xs[1::2])
     half = n // 2
     out = [None] * (half + 1)
@@ -74,11 +72,8 @@
 
 
 def irfft(spec, n):
-    if n == 3:
-        dc, (r, i) = spec[0][0], spec[1]
-        base = dc - r
-        t = i * np.sqrt(3.0)
-        return [dc + 2.0 * r, base - t, base + t]
+    if n == 1:
+        return [spec[0][0]]
     half = n // 2
     even, odd = [None] * (half // 2 + 1), [None] * (half // 2 + 1)
     for k in range(half // 2 + 1):
@@ -102,6 +97,36 @@
     out = [None] * n
     out[0::2], out[1::2] = ev, od
     return out
+
+
+def cfft(xs, sign):
+    n = len(xs)
+    if n == 1:
+        return xs
+    even, odd = cfft(xs[0::2], sign), cfft(xs[1::2], sign)
+    half = n // 2
+    out = [None] * n
+    for k in range(half):
+        (er, ei), (r, i) = even[k], odd[k]
+        if 4 * k == n:
+            out[k] = (er + i, ei - r) if sign < 0 else (er - i, ei + r)
+            out[k + half] = (er - i, ei + r) if sign < 0 else (er + i, ei - r)
+            continue
+        if k == 0:
+            tr, ti = r, i
+        else:
+            tr, ti = turn(r, i, np.cos(2 * np.pi * k / n), sign * np.sin(2 * np.pi * k / n))
+        out[k] = (er + tr, ei + ti)
+        out[k + half] = (er - tr, ei - ti)
+    return out
+
+
+def turn(r, i, c, s):
+    if abs(abs(c) - abs(s)) > 1e-9:
+        return r * c - i * s, r * s + i * c
+    if c * s > 0:
+        return (r - i) * c, (r + i) * c
+    return (r + i) * c, (i - r) * c
 
 
 def split(v):
@@ -417,12 +442,33 @@
         transform(blk, (jnp.where(i % 2 == 0, cross, far),), c)
 
     def conv(vals, kern):
-        spec = rfft(vals)
-        out = []
-        for k, (re, im) in enumerate(spec):
-            kv = kern(k)
-            out.append((re * kv, None if im is None else im * kv))
-        return irfft(out, ng)
+        n = len(vals)
+        m = n // 3
+        freq = {(k % 3, k % m): min(k, n - k) for k in range(n)}
+        real, pairs = [], []
+        for j in range(m):
+            a, b, c = (vals[(m * i + 3 * j) % n] for i in range(3))
+            s = b + c
+            real.append(a + s)
+            pairs.append((a - 0.5 * s, (c - b) * (np.sqrt(3.0) / 2)))
+        spec = []
+        for k, (re, im) in enumerate(rfft(real)):
+            kv = kern(freq[0, k])
+            spec.append((re * kv, None if im is None else im * kv))
+        real = irfft(spec, m)
+        spec = []
+        for k, (re, im) in enumerate(cfft(pairs, -1)):
+            kv = kern(freq[1, k])
+            spec.append((re * kv, im * kv))
+        pairs = cfft(spec, 1)
+        out = [None] * n
+        for j in range(m):
+            u, (re, im) = real[j], pairs[j]
+            base, t = u - re, im * np.sqrt(3.0)
+            out[3 * j % n] = u + (re + re)
+            out[(m + 3 * j) % n] = base - t
+            out[(2 * m + 3 * j) % n] = base + t
+        return out
 
     def xconv(t):
         order = [(g, h, r) for g in range(4) for h in range(2) for r in range(planes)]
@@ -514,7 +560,7 @@
         def _():
             load_k.wait()
 
-        lax.fori_loop(0, ng // 16, mid, 0)
+        lax.fori_loop(0, ng // 16, mid, 0, unroll=True)
         lax.fori_loop(0, 4, inv, 0)
         return 0
 
@@ -570,7 +616,7 @@
         def _():
             for c in range(2):
                 came(block, c)
-            columns(block, (me, sib, cross))
+            columns(block, (me, sib, cross, far))
 
         return 0
 
@@ -586,15 +632,11 @@
     settle(cross)
     spread_out(recv, cross, 2)
     lax.fori_loop(0, nband, early((cross,)), 0)
-    lax.fori_loop(0, nband, late, 0)
     settle(far)
     spread_out(recv, far, 3)
-
-    def last(block, _):
-        columns(block, (far,))
-        return 0
-
-    lax.fori_loop(0, nband, last, 0)
+    lax.fori_loop(0, nband, early((far,)), 0)
+    lax.fori_loop(0, nband, late, 0)
+
     lanes = jnp.sum(rows_buf[...], axis=2).reshape(groups * nband, width)
     left_over = lanes
     terms = jnp.zeros((groups * nband, 128), jnp.float32)

time: 54.2 us -> 54 us (level)
  no operation moved by 1% of the time
where the time goes in v7:
time: 54 us; the launch traced here: 53.9 us
  Pallas kernels  51.9 us (96%)
  local copies, waits for them, and re-layouts  1.34 us (2%)
  between operations  0.64 us (1%)
    pallas_call x1, Pallas kernels, solve(): pl.pallas_call(functools.partial(solve_kernel, ng, ng ** 3), out_shape=(j...  51.9 us
    unnamed x2, local copies, waits for them, and re-layouts  1.34 us

profile of v7, /device:TPU:0, one launch (start us, length us, event | category | flops | bytes accessed | tf_op | source)
XLA Modules:
  0.0 53.9 jit_solution(10888811406960098477)
XLA Ops:
  0.6 51.9 %solve.1 = (f32[216,4,128]{2,1,0:T(4,128)S(1)}, f32[4,8]{1,0:T(4,128)S(1)}) custom-call(f32[216,4,128]{2,1,0:T(4,128)} %bitcast.9, f32[25,72,128]{2,1,0:T(8,128)} %constant.4.clone.refs_0_, bf16[1968,256]{1,0:T(8,128)(2,1)} %constant.5.clone.refs_1_), custom_call_target="tpu_custom_call" | custom-call | flops 99999997952 | bytes 10000000 | tf_op jit(solution)/shard_map/solve/pallas_call | solution.py:747
  52.5 0.8 %copy.7 = f32[4,27648]{1,0:T(4,128)} copy(f32[4,27648]{1,0:T(4,128)S(1)} %bitcast.7) | data formatting | bytes 884736
  53.3 0.6 %copy.8 = f32[8,4]{0,1:T(4,128)} copy(f32[8,4]{0,1:T(4,128)S(1)} %bitcast.8) | data formatting | bytes 256

commit v8 on v7

--- a/solution.py
+++ b/solution.py
@@ -770,13 +770,34 @@
     )(nat, *[jnp.asarray(c) for c in consts])
 
 
+def leave_kernel(a_ref, b_ref, c_ref, d_ref, sems):
+    copies = [pltpu.make_async_copy(a_ref, c_ref, sems.at[0]), pltpu.make_async_copy(b_ref, d_ref, sems.at[1])]
+    for copy in copies:
+        copy.start()
+    for copy in copies:
+        copy.wait()
+
+
+def leave(a, b):
+    anywhere = pl.BlockSpec(memory_space=pl.ANY)
+    return pl.pallas_call(
+        leave_kernel,
+        out_shape=(jax.ShapeDtypeStruct(a.shape, a.dtype), jax.ShapeDtypeStruct(b.shape, b.dtype)),
+        in_specs=[pl.BlockSpec(memory_space=pltpu.VMEM)] * 2,
+        out_specs=(anywhere, anywhere),
+        scratch_shapes=[pltpu.SemaphoreType.DMA((2,))],
+        compiler_params=pltpu.CompilerParams(vmem_limit_bytes=1 << 20),
+        name="leave",
+    )(a, b)
+
+
 def on_device(orbitals):
     groups, nband = lax.axis_size("grid"), lax.axis_size("band")
     bands, local = orbitals.shape
     ncell = local * groups
     ng = round(ncell ** (1 / 3))
     nat = orbitals.reshape(bands, local // 128, 128).transpose(1, 0, 2)
-    out, marg = solve(nat, ng, groups, nband)
+    out, marg = leave(*solve(nat, ng, groups, nband))
     vectors = out.transpose(1, 0, 2).reshape(bands, local)
     margin = marg.T
     return (vectors, margin)

time: 54 us -> 53.5 us (level)
  local copies, waits for them, and re-layouts: 1.34 us -> 0 us
  Pallas kernels: 51.9 us -> 52.7 us
    unnamed x2 -> x0, local copies, waits for them, and re-layouts: 1.34 us -> none
    pallas_call x0 -> x1, Pallas kernels: none -> 0.78 us  [leave(): pl.pallas_call(leave_kernel, out_shape=(jax.ShapeDtypeStruct(a.shape, a.d...]
where the time goes in v8:
time: 53.5 us; the launch traced here: 53.3 us
  Pallas kernels  52.7 us (99%)
  between operations  0.64 us (1%)
    pallas_call x1, Pallas kernels, solve(): pl.pallas_call(functools.partial(solve_kernel, ng, ng ** 3), out_shape=(j...  51.9 us

profile of v8, /device:TPU:0, one launch (start us, length us, event | category | flops | bytes accessed | tf_op | source)
XLA Modules:
  0.0 53.3 jit_solution(13258656094767852503)
XLA Ops:
  0.6 51.9 %solve.1 = (f32[216,4,128]{2,1,0:T(4,128)S(1)}, f32[4,8]{1,0:T(4,128)S(1)}) custom-call(f32[216,4,128]{2,1,0:T(4,128)} %bitcast.7, f32[25,72,128]{2,1,0:T(8,128)} %constant.4.clone.refs_0_, bf16[1968,256]{1,0:T(8,128)(2,1)} %constant.5.clone.refs_1_), custom_call_target="tpu_custom_call" | custom-call | flops 99999997952 | bytes 10000000 | tf_op jit(solution)/shard_map/solve/pallas_call | solution.py:747
  52.5 0.8 %leave.1 = (f32[216,4,128]{2,1,0:T(4,128)}, f32[4,8]{1,0:T(4,128)}) custom-call(f32[216,4,128]{2,1,0:T(4,128)S(1)} %get-tuple-element.6.a_ref, f32[4,8]{1,0:T(4,128)S(1)} %get-tuple-element.7.b_ref), custom_call_target="tpu_custom_call" | custom-call | tf_op jit(solution)/shard_map/leave/pallas_call | solution.py:783

commit v9 on v8

--- a/solution.py
+++ b/solution.py
@@ -561,7 +561,7 @@
             load_k.wait()
 
         lax.fori_loop(0, ng // 16, mid, 0, unroll=True)
-        lax.fori_loop(0, 4, inv, 0)
+        lax.fori_loop(0, 4, inv, 0, unroll=True)
         return 0
 
     lax.fori_loop(0, 3, block, 0)
@@ -595,7 +595,7 @@
                 for n, p in zip(where, parts):
                     p[j] = p[j] + phi * ebuf[n, j, pl.ds(8 * r, 8)]
         for slot, p in zip(slots, parts):
-            rows_buf[slot, block] = jnp.concatenate(p, axis=1)
+            rows_buf[slot, pl.ds(block, 1), :] = jnp.sum(jnp.concatenate(p, axis=1), axis=0, keepdims=True)
 
     def ready(block):
         near_by = jnp.logical_or(block == pair, block == third)
@@ -637,7 +637,7 @@
     lax.fori_loop(0, nband, early((far,)), 0)
     lax.fori_loop(0, nband, late, 0)
 
-    lanes = jnp.sum(rows_buf[...], axis=2).reshape(groups * nband, width)
+    lanes = rows_buf[...].reshape(groups * nband, width)
     left_over = lanes
     terms = jnp.zeros((groups * nband, 128), jnp.float32)
     for _ in range(3):
@@ -756,7 +756,7 @@
             pltpu.VMEM(full[1:], f32), pltpu.VMEM((nband + 3 * groups,) + full[1:], f32),
             pltpu.VMEM(full, f32), pltpu.VMEM(full, f32), pltpu.VMEM((groups, flat // ng, ng, width), f32),
             pltpu.VMEM(slim, f32), pltpu.VMEM(slim, f32),
-            pltpu.VMEM((2, 256, 256), b16), pltpu.VMEM((groups, nband, 8, width), f32),
+            pltpu.VMEM((2, 256, 256), b16), pltpu.VMEM((groups, nband, width), f32),
             pltpu.VMEM((groups, groups, 128), f32), pltpu.VMEM((groups, groups, 128), f32),
             dma((3, groups - 1, 2)), dma((3,)), dma((nband, 2)), dma((nband // 2, 2)), dma((nband // 2, 2)), dma(()), dma(()),
             dma(()), dma((groups,)), dma(()), dma((groups,)), dma(()), dma((2,)), dma(()), dma((2,)),

time: 53.5 us -> 53.2 us (level)
  no operation moved by 1% of the time
where the time goes in v9:
time: 53.2 us; the launch traced here: 53 us
  Pallas kernels  52.4 us (98%)
  between operations  0.64 us (1%)
    pallas_call x1, Pallas kernels, solve(): pl.pallas_call(functools.partial(solve_kernel, ng, ng ** 3), out_shape=(j...  51.6 us

profile of v9, /device:TPU:0, one launch (start us, length us, event | category | flops | bytes accessed | tf_op | source)
XLA Modules:
  0.0 53.0 jit_solution(5939394801672701749)
XLA Ops:
  0.6 51.6 %solve.1 = (f32[216,4,128]{2,1,0:T(4,128)S(1)}, f32[4,8]{1,0:T(4,128)S(1)}) custom-call(f32[216,4,128]{2,1,0:T(4,128)} %bitcast.7, f32[25,72,128]{2,1,0:T(8,128)} %constant.4.clone.refs_0_, bf16[1968,256]{1,0:T(8,128)(2,1)} %constant.5.clone.refs_1_), custom_call_target="tpu_custom_call" | custom-call | flops 99999997952 | bytes 10000000 | tf_op jit(solution)/shard_map/solve/pallas_call | solution.py:747
  52.2 0.8 %leave.1 = (f32[216,4,128]{2,1,0:T(4,128)}, f32[4,8]{1,0:T(4,128)}) custom-call(f32[216,4,128]{2,1,0:T(4,128)S(1)} %get-tuple-element.6.a_ref, f32[4,8]{1,0:T(4,128)S(1)} %get-tuple-element.7.b_ref), custom_call_target="tpu_custom_call" | custom-call | tf_op jit(solution)/shard_map/leave/pallas_call | solution.py:783
